TPU v7x, 32 devices: a whole 2x2x4 slice. The times are simulated.
32 devices in a mesh: groups: 2 (over y), pool: 8 (over z, x), heads: 2 (over core).
Axes of the slice: x: 2, y: 2, z: 4, core: 2. Of those that a mesh axis runs over, the one named last changes fastest.
Arguments:
- hidden_in: bfloat16 [32, 8192], P('groups'), parts along dimension 0, may hold values from -50 to 50
- key_cache: bfloat16 [32, 8, 4096, 128], P('groups', 'heads', 'pool'), parts along dimension 0, may hold values from -200 to 200
- value_cache: bfloat16 [32, 8, 4096, 128], P('groups', 'heads', 'pool'), parts along dimension 0, may hold values from -6 to 6
- positions: int32 [3, 32, 4096], P(None, 'groups', 'pool'), parts along dimension 1, may hold values from 0 to 4095, as said below
- query_pos: int32 [3, 32], P(None, 'groups'), parts along dimension 1, may hold values from 4096 to 8207
- lengths: int32 [32], P('groups'), parts along dimension 0, may hold values from 1024 to 4096, as said below
- query_weight: bfloat16 [8192, 8192], P('pool', 'heads'), may hold values from -0.0625 to 0.0625
- key_weight: bfloat16 [8192, 1024], P('pool', 'heads'), may hold values from -0.16503906 to 0.16503906
- value_weight: bfloat16 [8192, 1024], P('pool', 'heads'), may hold values from -0.16503906 to 0.16503906
- out_weight: bfloat16 [8192, 8192], P('heads', 'pool'), may hold values from -0.5 to 0.5
- gate_weight: bfloat16 [8192, 14848], P(None, ('pool', 'heads')), may hold values from -0.0625 to 0.0625
- up_weight: bfloat16 [8192, 14848], P(None, ('pool', 'heads')), may hold values from -0.0625 to 0.0625
- down_weight: bfloat16 [14848, 8192], P(('pool', 'heads')), may hold values from -0.0625 to 0.0625
Outputs:
- output: bfloat16 [32, 8192], P('groups', 'pool'), parts along dimension 0
There are 2 independent parts, one for each index of `groups`. A program takes and returns all parts, laid end to end along the dimension named above; an argument that names none is the same for every part. Nothing has to cross between parts.
Inputs may be any that keep to these rules, and one draw needn't show every extreme that they name: `positions`: text tokens carry three equal ids; one prompt is text only. `lengths`: some prompt fills all 4096 slots.
All inputs are finite; a program needn't handle non-finite values.
Results may differ from a plain program's by a relative error of at most 0.007.
The roundings to bfloat16 on the way count: a program that leaves them out, or rounds other values in their place, can miss the bound.
Values may be sent and summed in bfloat16 or wider, within the bound.
No kernel may reach another device: no remote copies, remote signals or barrier semaphores. Data moves between devices by JAX's collectives and lax.ppermute only.
A program may use at most 192 MiB of HBM per device.

v0:
```python
import math

import jax
import jax.numpy as jnp
from jax import lax
from jax.sharding import PartitionSpec as P

D = 8192
HEADS = 64
KV_HEADS = 8
HD = 128
PROMPTS = 16


EPS = 1e-06
THETA = 1000000.0


def angle_tables(triple):
    half_dim = HD // 2
    column = jnp.arange(half_dim)
    first_end = HD // 8
    second_end = first_end + 3 * HD // 16
    chosen = jnp.where(
        column < first_end,
        triple[0][..., None],
        jnp.where(column < second_end, triple[1][..., None], triple[2][..., None]),
    )
    inverse = jnp.exp(column.astype(jnp.float32) * (-2.0 * math.log(THETA) / HD))
    angles = chosen.astype(jnp.float32) * inverse
    return (jnp.cos(angles), jnp.sin(angles))


def rotate(values, cos_table, sin_table):
    half_dim = values.shape[-1] // 2
    lower_half = values[..., :half_dim]
    upper_half = values[..., half_dim:]
    return jnp.concatenate(
        [
            lower_half * cos_table - upper_half * sin_table,
            upper_half * cos_table + lower_half * sin_table,
        ],
        -1,
    )


def normalize(values):
    return values * lax.rsqrt(jnp.mean(values * values, -1, keepdims=True) + EPS)


def prepare(projected_rows, item_ids, local_heads, query_pos):
    query_width = projected_rows.shape[1] - 2 * HD
    prompt_ids = item_ids // local_heads
    triple = query_pos[:, prompt_ids]
    cos_table, sin_table = angle_tables(triple)
    item_count = projected_rows.shape[0]
    raw_queries = projected_rows[:, :query_width].reshape(item_count, query_width // HD, HD)
    queries = rotate(raw_queries, cos_table[:, None], sin_table[:, None]).astype(jnp.bfloat16)
    own_keys = rotate(
        projected_rows[:, query_width : query_width + HD], cos_table, sin_table
    ).astype(jnp.bfloat16)
    own_values = projected_rows[:, query_width + HD :].astype(jnp.bfloat16)
    return (queries, own_keys, own_values)


def partial_softmax(queries, key_rows, value_rows, item_lengths, offset):
    scores = jnp.einsum(
        "igd,isd->igs", queries, key_rows, preferred_element_type=jnp.float32
    ) * HD ** (-0.5)
    slot_index = offset + jnp.arange(key_rows.shape[1])
    valid_mask = slot_index[None, None, :] < item_lengths[:, None, None]
    scores = jnp.where(valid_mask, scores, -1e30)
    peak_score = jnp.max(scores, -1)
    weights = jnp.where(valid_mask, jnp.exp(scores - peak_score[..., None]), 0.0)
    weighted = jnp.einsum("igs,isd->igd", weights, value_rows.astype(jnp.float32))
    return (peak_score, jnp.sum(weights, -1), weighted.reshape(queries.shape[0], -1))


def combine(peaks, totals, weighted, own_score, own_values):
    item_count, source_count, group_size = peaks.shape
    top_score = jnp.maximum(jnp.max(peaks, 1), own_score)
    factor = jnp.exp(peaks - top_score[:, None])
    own_weight = jnp.exp(own_score - top_score)
    denominator = jnp.sum(totals * factor, 1) + own_weight
    numerator = jnp.sum(
        weighted.reshape(item_count, source_count, group_size, HD) * factor[..., None], 1
    )
    numerator = numerator + own_weight[..., None] * own_values.astype(jnp.float32)[:, None, :]
    return (
        (numerator / denominator[..., None])
        .reshape(item_count, group_size * HD)
        .astype(jnp.bfloat16)
    )


def per_device(
    hidden_in,
    key_cache,
    value_cache,
    positions,
    query_pos,
    lengths,
    query_weight,
    key_weight,
    value_weight,
    out_weight,
    gate_weight,
    up_weight,
    down_weight,
):
    pool_index = lax.axis_index("pool")
    pool_size = lax.axis_size("pool")
    local_heads = key_cache.shape[1]
    group_size = HEADS // KV_HEADS
    query_width = group_size * HD
    all_items = PROMPTS * local_heads
    my_count = all_items // pool_size
    my_start = pool_index * my_count
    seq_local = key_cache.shape[2]
    block_cols = D // pool_size
    normed = normalize(hidden_in.astype(jnp.float32)).astype(jnp.bfloat16)
    normed_cols = lax.dynamic_slice_in_dim(normed, pool_index * block_cols, block_cols, 1)
    term = jnp.concatenate(
        [
            jnp.dot(normed_cols, query_weight, preferred_element_type=jnp.float32).reshape(
                PROMPTS, local_heads, query_width
            ),
            jnp.dot(normed_cols, key_weight, preferred_element_type=jnp.float32).reshape(
                PROMPTS, local_heads, HD
            ),
            jnp.dot(normed_cols, value_weight, preferred_element_type=jnp.float32).reshape(
                PROMPTS, local_heads, HD
            ),
        ],
        2,
    ).reshape(all_items, query_width + 2 * HD)
    cos_table, sin_table = angle_tables(positions)
    rotated = rotate(key_cache.astype(jnp.float32), cos_table[:, None], sin_table[:, None]).astype(
        jnp.bfloat16
    )
    rotated = rotated.reshape(all_items, seq_local, HD)
    value_rows = value_cache.reshape(all_items, seq_local, HD)
    item_lengths = jnp.repeat(lengths, local_heads)
    projected_all = lax.psum(term, "pool")
    all_queries, all_keys, all_values = prepare(
        projected_all, jnp.arange(all_items), local_heads, query_pos
    )
    local_peaks, local_totals, local_weighted = partial_softmax(
        all_queries, rotated, value_rows, item_lengths, pool_index * seq_local
    )
    peaks, totals, weighted = (
        lax.all_to_all(local_peaks[:, None], "pool", split_axis=0, concat_axis=1, tiled=True),
        lax.all_to_all(local_totals[:, None], "pool", split_axis=0, concat_axis=1, tiled=True),
        lax.all_to_all(local_weighted[:, None], "pool", split_axis=0, concat_axis=1, tiled=True),
    )
    queries = lax.dynamic_slice_in_dim(all_queries, my_start, my_count, 0)
    own_keys = lax.dynamic_slice_in_dim(all_keys, my_start, my_count, 0)
    own_values = lax.dynamic_slice_in_dim(all_values, my_start, my_count, 0)
    own_score = jnp.einsum(
        "igd,id->ig", queries, own_keys, preferred_element_type=jnp.float32
    ) * HD ** (-0.5)
    attended = combine(peaks, totals, weighted, own_score, own_values)
    gathered = lax.all_gather(attended, "pool", axis=0, tiled=True).reshape(
        PROMPTS, local_heads * query_width
    )
    attn_out = lax.psum(jnp.dot(gathered, out_weight, preferred_element_type=jnp.float32), "heads")
    hidden_cols = lax.dynamic_slice_in_dim(hidden_in, pool_index * block_cols, block_cols, 1)
    mid_state = (hidden_cols.astype(jnp.float32) + attn_out).astype(jnp.bfloat16)
    squares = lax.psum(jnp.sum(jnp.square(mid_state.astype(jnp.float32)), -1), "pool")
    whole_state = lax.all_gather(mid_state, "pool", axis=1, tiled=True)
    inverse = lax.rsqrt(squares / D + EPS)
    normed_state = (whole_state.astype(jnp.float32) * inverse[:, None]).astype(jnp.bfloat16)
    gate_values = jnp.dot(normed_state, gate_weight, preferred_element_type=jnp.float32)
    up_values = jnp.dot(normed_state, up_weight, preferred_element_type=jnp.float32)
    active = (jax.nn.silu(gate_values) * up_values).astype(jnp.bfloat16)
    partial_out = jnp.dot(active, down_weight, preferred_element_type=jnp.float32)
    mlp_cols = lax.psum_scatter(partial_out, "pool", scatter_dimension=1, tiled=True)
    mlp_cols = lax.psum(mlp_cols, "heads")
    return (mid_state.astype(jnp.float32) + mlp_cols).astype(jnp.bfloat16)


def solution(mesh):
    in_specs = (
        P("groups", None),
        P("groups", "heads", "pool", None),
        P("groups", "heads", "pool", None),
        P(None, "groups", "pool"),
        P(None, "groups"),
        P("groups"),
        P("pool", "heads"),
        P("pool", "heads"),
        P("pool", "heads"),
        P("heads", "pool"),
        P(None, ("pool", "heads")),
        P(None, ("pool", "heads")),
        P(("pool", "heads"), None),
    )
    out_specs = P("groups", "pool")
    return jax.shard_map(
        per_device, mesh=mesh, in_specs=in_specs, out_specs=out_specs, check_vma=False
    )
```

profile of v0, /device:TPU:0, one launch (start us, length us, event | category | flops | bytes accessed | tf_op | source)
XLA Modules:
  0.0 357.5 jit_solution(8407712216756091066)
XLA Ops:
  6.5 0.0 copy-start
  6.5 0.0 all-reduce.4.cloned.1.call-start
  6.5 1.1 convert_element_type.78
  7.6 1.1 multiply_reduce_fusion
  8.8 0.0 copy-done
  8.8 0.3 fusion.54
  9.1 1.5 fusion.50
  10.6 4.6 %fusion.52 = f32[16,4096]{1,0:T(8,128)S(1)} fusion(bf16[1024,4096]{1,0:T(8,128)(2,1)} %param.19, f32[16,8192]{1,0:T(8,128)S(1)} %convert_element_type.78, s32[]{:T(128)S(6)} %select_n.82, f32[16]{0:T(128)S(1)} %add_rsqrt_fusion.1), kind=kOutput, calls=%fused_computation.96 | convolution fusion | flops 134250496 | bytes 8716804 | tf_op jit(solution)/shard_map/dot_general | solution.py:125
  15.2 0.1 concatenate.27
  15.3 0.7 pad_maximum_fusion
  16.0 0.0 all-reduce.4.cloned.1.call-update
  16.1 0.0 copy-start.2
  16.1 0.0 copy-start.3
  16.1 0.0 copy-start.4
  16.1 11.3 %convert_element_type.82 = f32[16,4,512,128]{3,2,1,0:T(8,128)} convert(bf16[16,4,512,128]{3,2,1,0:T(8,128)(2,1)} %param.14) | non-fusion elementwise | flops 4194304 | bytes 25165824 | tf_op jit(solution)/shard_map/convert_element_type | solution.py:138
  27.5 0.0 copy-done.2
  27.5 0.0 copy-done.3
  27.5 0.1 copy.22
  27.6 0.6 gather_fusion
  28.2 0.2 slice_reduce_fusion.2
  28.4 0.1 broadcast_in_dim.119
  28.5 0.1 lt.54
  28.5 42.2 %fusion.5 = (f32[16,512,64]{2,1,0:T(8,128)S(1)}, f32[16,512,64]{2,1,0:T(8,128)S(1)}) fusion(f32[64]{0:T(128)S(1)} %multiply_exponential_fusion, s32[16,512]{1,0:T(8,128)S(1)} %get-tuple-element.23, s32[16,512]{1,0:T(8,128)S(1)} %get-tuple-element.24, s32[16,512]{1,0:T(8,128)S(1)} %get-tuple-element.22, pred[64]{0:T(512)(128)(4,1)S(1)} %get-tuple-element.29, ...), kind=kLoop, calls=%fused_computation.9 | loop fusion | flops 2097152 | bytes 4292992 | tf_op jit(solution)/shard_map/cos | solution.py:31
  70.7 19.2 %subtract_convert_fusion = (bf16[16,4,512,64]{3,2,1,0:T(8,128)(2,1)}, bf16[16,4,512,64]{3,2,1,0:T(8,128)(2,1)}) fusion(f32[16,4,512,128]{3,2,1,0:T(8,128)} %convert_element_type.82, f32[16,512,64]{2,1,0:T(8,128)S(1)} %get-tuple-element.21, f32[16,512,64]{2,1,0:T(8,128)S(1)} %get-tuple-element.20), kind=kLoop, calls=%fused_computation.2 | loop fusion | flops 16777216 | bytes 29360128 | tf_op jit(solution)/shard_map/convert.6
  90.0 0.1 broadcast_compare_fusion
  90.1 0.2 all-reduce.4.cloned.1.call-done
  90.3 1.0 slice_bitcast_fusion
  91.3 1.1 subtract_convert_fusion.2
  92.4 0.2 subtract_convert_fusion.1
  92.6 9.3 %fusion.49 = (f32[64,8]{1,0:T(8,128)}, f32[64,8,512]{2,1,0:T(8,128)S(1)}) fusion(bf16[64,512,64]{2,1,0:T(8,128)(2,1)} %bitcast.54, bf16[64,512,64]{2,1,0:T(8,128)(2,1)} %bitcast.53, bf16[64,8,64]{2,1,0:T(8,128)(2,1)S(1)} %get-tuple-element.19, bf16[64,8,64]{2,1,0:T(8,128)(2,1)S(1)} %get-tuple-element.18, pred[64,512]{1,0:T(8,128)(4,1)S(1)} %broadcast_compare_fusion), kind=kOutput, calls=%fused_computation.94 | convolution fusion | flops 84934144 | bytes 9603072 | tf_op jit(solution)/shard_map/igd,isd->igs/dot_general | solution.py:67
  101.9 7.1 %all-to-all-start.1 = ((f32[64,1,8]{2,1,0:T(1,128)}), f32[64,1,8]{2,1,0:T(1,128)S(1)}, u32[]{:S(2)}, u32[]{:S(2)}) async-start(f32[64,1,8]{2,1,0:T(1,128)} %bitcast.11), calls=%async_computation.1 | async-start | bytes 65536 | tf_op jit(solution)/shard_map/all_to_all | solution.py:152
  108.9 0.1 fusion.41
  109.0 0.2 fusion.36
  109.2 5.4 %fusion.14 = f32[64,8,128]{2,1,0:T(8,128)} fusion(bf16[64,512,128]{2,1,0:T(8,128)(2,1)} %bitcast.55, f32[64,8,512]{2,1,0:T(8,128)S(1)} %get-tuple-element.28, f32[64,8]{1,0:T(8,128)} %get-tuple-element.27, pred[64,512]{1,0:T(8,128)(4,1)S(1)} %broadcast_compare_fusion), kind=kOutput, calls=%fused_computation.16 | convolution fusion | flops 67633152 | bytes 9734144 | tf_op jit(solution)/shard_map/igs,isd->igd/dot_general | solution.py:75
  114.5 1.7 fusion.13
  116.3 0.8 slice.72
  117.1 0.0 all-to-all-done.1
  117.1 6.0 %all-to-all-start.2 = ((f32[64,1,8]{2,1,0:T(1,128)}), f32[64,1,8]{2,1,0:T(1,128)S(1)}, u32[]{:S(2)}, u32[]{:S(2)}) async-start(f32[64,1,8]{2,1,0:T(1,128)} %bitcast.21), calls=%async_computation.2 | async-start | bytes 65536 | tf_op jit(solution)/shard_map/all_to_all | solution.py:153
  123.1 6.7 %all-to-all-done.2 = f32[64,1,8]{2,1,0:T(1,128)S(1)} async-done(((f32[64,1,8]{2,1,0:T(1,128)}), f32[64,1,8]{2,1,0:T(1,128)S(1)}, u32[]{:S(2)}, u32[]{:S(2)}) %all-to-all-start.2) | async-done | bytes 2080 | tf_op jit(solution)/shard_map/all_to_all | solution.py:153
  129.7 3.4 all-to-all-start
  133.2 0.0 all-reduce.6.cloned.1.call-start
  133.3 0.1 copy.25
  133.3 0.1 copy.24
  133.4 7.9 %all-to-all-done = f32[64,1,1024]{2,1,0:T(1,128)S(1)} async-done(((f32[64,1,1024]{2,1,0:T(1,128)}), f32[64,1,1024]{2,1,0:T(1,128)S(1)}, u32[]{:S(2)}, u32[]{:S(2)}) %all-to-all-start) | async-done | bytes 262176 | tf_op jit(solution)/shard_map/all_to_all | solution.py:154
  141.3 0.1 mul.222
  141.4 0.4 multiply_reduce_fusion.1
  141.8 0.1 fusion.31
  141.9 30.6 %all_gather.6 = bf16[64,1024]{1,0:T(8,128)(2,1)S(1)} all-gather(bf16[8,1024]{1,0:T(8,128)(2,1)S(1)} %fusion.31), channel_id=1, replica_groups=mesh['groups'=2,'pool'=8,'heads'=2] {'pool'}, dimensions={0}, use_global_device_ids=true | all-gather | bytes 147456 | tf_op jit(solution)/shard_map/all_gather | solution.py:163
  172.5 0.1 reshape.304
  172.6 5.2 %fusion.56 = f32[16,1024]{1,0:T(8,128)} fusion(bf16[16,4096]{1,0:T(8,128)(2,1)S(1)} %reshape.304, bf16[4096,1024]{1,0:T(8,128)(2,1)} %param.22), kind=kOutput, calls=%fused_computation.98 | convolution fusion | flops 134217728 | bytes 8585216 | tf_op jit(solution)/shard_map/dot_general | solution.py:166
  177.8 0.0 all-reduce.6.cloned.1.call-update
  177.8 0.0 reduce-scatter.2.cloned.1.call-start
  177.8 16.1 %all-reduce.6.cloned.1.call-done = f32[16,1024]{1,0:T(8,128)} async-done(((f32[16,1024]{1,0:T(8,128)}), f32[16,1024]{1,0:T(8,128)}) %all-reduce.6.cloned.1.call-update) | async-done | bytes 65552 | tf_op jit(solution)/shard_map/psum | solution.py:166
  193.9 1.0 fusion.23
  194.9 31.1 %all_gather.7 = bf16[16,8192]{1,0:T(8,128)(2,1)S(1)} all-gather(bf16[16,1024]{1,0:T(8,128)(2,1)S(1)} %get-tuple-element.9), channel_id=1, replica_groups=mesh['groups'=2,'pool'=8,'heads'=2] {'pool'}, dimensions={1}, use_global_device_ids=true | all-gather | bytes 294912 | tf_op jit(solution)/shard_map/all_gather | solution.py:170
  226.0 21.3 %psum.30 = f32[16]{0:T(128)S(1)} all-reduce(f32[16]{0:T(128)S(1)} %get-tuple-element.8), channel_id=1, replica_groups=mesh['groups'=2,'pool'=8,'heads'=2] {'pool'}, use_global_device_ids=true, to_apply=%region_9.10 | all-reduce | flops 16 | bytes 128 | tf_op jit(solution)/shard_map/psum | solution.py:169
  247.3 9.4 %fusion.22 = f32[16,928]{1,0:T(8,128)S(1)} fusion(bf16[8192,928]{0,1:T(8,128)(2,1)} %param.23, bf16[16,8192]{1,0:T(8,128)(2,1)S(1)} %all_gather.7, f32[16]{0:T(128)S(1)} %add_rsqrt_fusion), kind=kOutput, calls=%fused_computation.33 | convolution fusion | flops 243662848 | bytes 15525952 | tf_op jit(solution)/shard_map/dot_general | solution.py:173
  256.7 13.9 %fusion.15 = f32[16,8192]{1,0:T(8,128)} fusion(bf16[928,8192]{1,0:T(8,128)(2,1)} %param.25, bf16[8192,928]{0,1:T(8,128)(2,1)} %param.24, bf16[16,8192]{1,0:T(8,128)(2,1)S(1)} %all_gather.7, f32[16]{0:T(128)S(1)} %add_rsqrt_fusion, f32[16,928]{1,0:T(8,128)S(1)} %fusion.22), kind=kOutput, calls=%fused_computation.17 | convolution fusion | flops 487021568 | bytes 31254592 | tf_op jit(solution)/shard_map/dot_general | solution.py:176
  270.6 0.0 reduce-scatter.2.cloned.1.call-update
  270.7 0.0 all-reduce.8.cloned.1.call-start
  270.7 60.0 %reduce-scatter.2.cloned.1.call-done = f32[16,1024]{1,0:T(8,128)} async-done(((f32[16,8192]{1,0:T(8,128)}), f32[16,1024]{1,0:T(8,128)}) %reduce-scatter.2.cloned.1.call-update) | async-done | bytes 65552 | tf_op jit(solution)/shard_map/reduce_scatter | solution.py:177
  330.7 0.0 all-reduce.8.cloned.1.call-update
  330.7 18.8 %all-reduce.8.cloned.1.call-done = f32[16,1024]{1,0:T(8,128)} async-done(((f32[16,1024]{1,0:T(8,128)}), f32[16,1024]{1,0:T(8,128)}) %all-reduce.8.cloned.1.call-update) | async-done | bytes 65552 | tf_op jit(solution)/shard_map/psum | solution.py:178
  349.5 1.5 fusion.24
  (19 shorter events, 0.2 us)
Async XLA Ops:
  6.5 2.2 copy-start
  6.5 83.8 %all-reduce.4.cloned.1.call-start = ((), (), s32[]{:S(2)}) async-start(), calls=%async_computation.4 | async-start | bytes 655360 | tf_op jit(solution)/shard_map/psum | solution.py:144
  16.1 11.4 %copy-start.2 = (s32[3,16,512]{2,1,0:T(8,128)S(1)}, s32[3,16,512]{2,1,0:T(8,128)}, u32[]{:S(2)}) copy-start(s32[3,16,512]{2,1,0:T(8,128)} %param.16) | copy-start | bytes 294916
  16.1 11.4 %copy-start.3 = (s32[3,16]{1,0:T(4,128)S(1)}, s32[3,16]{1,0:T(4,128)}, u32[]{:S(2)}) copy-start(s32[3,16]{1,0:T(4,128)} %param.17) | copy-start | bytes 580
  16.1 12.2 %copy-start.4 = (s32[16]{0:T(128)S(1)}, s32[16]{0:T(128)}, u32[]{:S(2)}) copy-start(s32[16]{0:T(128)} %param.18) | copy-start | bytes 196
  101.9 15.2 %all-to-all-start.1 = ((f32[64,1,8]{2,1,0:T(1,128)}), f32[64,1,8]{2,1,0:T(1,128)S(1)}, u32[]{:S(2)}, u32[]{:S(2)}) async-start(f32[64,1,8]{2,1,0:T(1,128)} %bitcast.11), calls=%async_computation.1 | async-start | bytes 65536 | tf_op jit(solution)/shard_map/all_to_all | solution.py:152
  117.1 12.7 %all-to-all-start.2 = ((f32[64,1,8]{2,1,0:T(1,128)}), f32[64,1,8]{2,1,0:T(1,128)S(1)}, u32[]{:S(2)}, u32[]{:S(2)}) async-start(f32[64,1,8]{2,1,0:T(1,128)} %bitcast.21), calls=%async_computation.2 | async-start | bytes 65536 | tf_op jit(solution)/shard_map/all_to_all | solution.py:153
  129.7 11.6 %all-to-all-start = ((f32[64,1,1024]{2,1,0:T(1,128)}), f32[64,1,1024]{2,1,0:T(1,128)S(1)}, u32[]{:S(2)}, u32[]{:S(2)}) async-start(f32[64,1,1024]{2,1,0:T(1,128)} %bitcast.8), calls=%async_computation | async-start | bytes 524288 | tf_op jit(solution)/shard_map/all_to_all | solution.py:154
  133.2 60.8 %all-reduce.6.cloned.1.call-start = ((), (), s32[]{:S(2)}) async-start(), calls=%async_computation.5 | async-start | bytes 131072 | tf_op jit(solution)/shard_map/psum | solution.py:166
  177.8 152.9 %reduce-scatter.2.cloned.1.call-start = ((), (), s32[]{:S(2)}) async-start(), calls=%async_computation.6 | async-start | bytes 589824 | tf_op jit(solution)/shard_map/reduce_scatter | solution.py:177
  247.3 103.7 %copy-start.1 = (bf16[1024,512]{1,0:T(8,128)(2,1)S(1)}, bf16[1024,512]{1,0:T(8,128)(2,1)}, u32[]{:S(2)}) copy-start(bf16[1024,512]{1,0:T(8,128)(2,1)} %param.21) | copy-start | bytes 3145732
  270.7 78.9 %all-reduce.8.cloned.1.call-start = ((), (), s32[]{:S(2)}) async-start(), calls=%async_computation.7 | async-start | bytes 131072 | tf_op jit(solution)/shard_map/psum | solution.py:178
Sparse Core Ops, SparseCore 0:
  16.2 74.0 all-reduce.3
  177.9 15.9 all-reduce.5
  270.8 59.8 reduce-scatter.1
  332.8 16.6 all-reduce.7
where the time goes:
time: 358 us
  waiting for transfers between devices  110 us (31%)
  blocking collectives  82.9 us (23%)
  other arithmetic  81.8 us (23%)
  matrix products  49.8 us (14%)
  starting transfers between devices  16.6 us (5%)
  between operations  13.3 us (4%)
    reduce_scatter x1, waiting for transfers between devices, per_device(): lax.psum_scatter(partial_out, 'pool', scatter_dimension=1, tiled=True)  60 us
    cos x1, other arithmetic, angle_tables(): return (jnp.cos(angles), jnp.sin(angles))  42.2 us
    all_gather x1, blocking collectives, per_device(): whole_state = lax.all_gather(mid_state, 'pool', axis=1, tiled=True)  31.1 us
    all_gather x1, blocking collectives, per_device(): lax.all_gather(attended, 'pool', axis=0, tiled=True)  30.6 us
    psum x1, blocking collectives, per_device(): lax.psum(jnp.sum(jnp.square(mid_state.astype(jnp.float32)), -1), 'pool')  21.3 us
    another operation x3, other arithmetic  20.5 us
    psum x1, waiting for transfers between devices, per_device(): mlp_cols = lax.psum(mlp_cols, 'heads')  18.8 us
    psum x1, waiting for transfers between devices, per_device(): lax.psum(jnp.dot(gathered, out_weight, preferred_element_type=jnp.float32...  16.1 us
  transfers between devices with their start and end apart: 7, of which 6 were waited for; matrix products, arithmetic and copies ran while one was open for 23% of the time, Pallas kernels for 0%

commit v1 on v0

v1 whole, which is shorter than its diff:
```python
import math

import jax
import jax.numpy as jnp
from jax import lax
from jax.sharding import PartitionSpec as P

HD = 128
EPS = 1e-06
THETA = 1000000.0
NEG = -1e30


def sin_cos(angles):
    turns = (angles * (2.0 / math.pi) + 0.5).astype(jnp.int32)
    count = turns.astype(jnp.float32)
    rest = angles - count * 1.5703125
    rest = rest - count * 4.837512969970703125e-4
    rest = rest - count * 7.54978995489188216e-8
    square = rest * rest
    sine = ((-1.9515295891e-4 * square + 8.3321608736e-3) * square - 1.6666654611e-1) * square * rest + rest
    cosine = (
        ((2.443315711809948e-5 * square - 1.388731625493765e-3) * square + 4.166664568298827e-2) * square * square
        - 0.5 * square
        + 1.0
    )
    odd = (turns & 1) == 1
    sin_out = jnp.where(odd, cosine, sine)
    cos_out = jnp.where(odd, sine, cosine)
    sin_out = jnp.where((turns & 2) == 2, -sin_out, sin_out)
    cos_out = jnp.where(((turns + 1) & 2) == 2, -cos_out, cos_out)
    return sin_out, cos_out


def angle_tables(triple):
    half_dim = HD // 2
    column = jnp.arange(half_dim)
    first_end = HD // 8
    second_end = first_end + 3 * HD // 16
    chosen = jnp.where(
        column < first_end,
        triple[0][..., None],
        jnp.where(column < second_end, triple[1][..., None], triple[2][..., None]),
    )
    inverse = jnp.exp(column.astype(jnp.float32) * (-2.0 * math.log(THETA) / HD))
    sine, cosine = sin_cos(chosen.astype(jnp.float32) * inverse)
    return cosine, sine


def rotate(values, cos_table, sin_table):
    half_dim = values.shape[-1] // 2
    lower_half = values[..., :half_dim]
    upper_half = values[..., half_dim:]
    return jnp.concatenate(
        [
            lower_half * cos_table - upper_half * sin_table,
            upper_half * cos_table + lower_half * sin_table,
        ],
        -1,
    )


def exchange(pieces):
    return lax.all_to_all(pieces, "pool", 0, 0, tiled=True)


def gather(block):
    pool_size = lax.axis_size("pool")
    return exchange(jnp.broadcast_to(block[None], (pool_size,) + block.shape))


def heads_sum(values):
    size = lax.axis_size("heads")
    total = values
    moved = values
    for _ in range(size - 1):
        moved = lax.ppermute(moved, "heads", [(k, (k + 1) % size) for k in range(size)])
        total = total + moved
    return total


def per_device(
    hidden_in,
    key_cache,
    value_cache,
    positions,
    query_pos,
    lengths,
    query_weight,
    key_weight,
    value_weight,
    out_weight,
    gate_weight,
    up_weight,
    down_weight,
):
    pool_index = lax.axis_index("pool")
    pool_size = lax.axis_size("pool")
    prompts, width = hidden_in.shape
    local_heads, seq_local = key_cache.shape[1:3]
    query_width = query_weight.shape[1] // local_heads
    group_size = query_width // HD
    all_items = prompts * local_heads
    my_count = all_items // pool_size
    my_start = pool_index * my_count
    block_cols = width // pool_size
    scale = HD ** (-0.5)

    squares = jnp.sum(jnp.square(hidden_in.astype(jnp.float32)), -1, keepdims=True)
    hidden_cols = lax.dynamic_slice_in_dim(hidden_in, pool_index * block_cols, block_cols, 1)
    normed_cols = (hidden_cols.astype(jnp.float32) * lax.rsqrt(squares / width + EPS)).astype(jnp.bfloat16)
    term = jnp.concatenate(
        [
            jnp.dot(normed_cols, weight, preferred_element_type=jnp.float32).reshape(prompts, local_heads, -1)
            for weight in (query_weight, key_weight, value_weight)
        ],
        2,
    ).reshape(pool_size, my_count, query_width + 2 * HD)
    received = exchange(term)

    cos_table, sin_table = angle_tables(positions)
    rotated = rotate(key_cache.astype(jnp.float32), cos_table[:, None], sin_table[:, None]).astype(jnp.bfloat16)
    rotated = rotated.reshape(all_items, seq_local, HD)
    value_rows = value_cache.reshape(all_items, seq_local, HD)
    item_lengths = jnp.repeat(lengths, local_heads)

    projected = jnp.sum(received, 0).reshape(my_count, group_size + 2, HD)
    my_prompts = (my_start + jnp.arange(my_count)) // local_heads
    my_cos, my_sin = angle_tables(query_pos[:, my_prompts])
    turned = rotate(projected[:, : group_size + 1], my_cos[:, None], my_sin[:, None])
    mine = jnp.concatenate([turned, projected[:, group_size + 1 :]], 1).astype(jnp.bfloat16)
    everything = gather(mine).reshape(all_items, group_size + 2, HD)
    queries = everything[:, :group_size]
    own_keys = everything[:, group_size]
    own_values = everything[:, group_size + 1].astype(jnp.float32)

    scores = jnp.einsum("igd,isd->igs", queries, rotated, preferred_element_type=jnp.float32) * scale
    slot_index = pool_index * seq_local + jnp.arange(seq_local)
    valid_mask = slot_index[None, None, :] < item_lengths[:, None, None]
    scores = jnp.where(valid_mask, scores, NEG)
    own_score = jnp.einsum("igd,id->ig", queries, own_keys, preferred_element_type=jnp.float32) * scale
    own_score = jnp.where(pool_index == 0, own_score, NEG)
    peak = jnp.maximum(jnp.max(scores, -1), own_score)
    weights = jnp.where(valid_mask, jnp.exp(scores - peak[..., None]), 0.0)
    own_weight = jnp.where(pool_index == 0, jnp.exp(own_score - peak), 0.0)
    total = jnp.sum(weights, -1) + own_weight
    weighted = jnp.einsum("igs,isd->igd", weights, value_rows.astype(jnp.float32))
    weighted = weighted + own_weight[..., None] * own_values[:, None, :]
    safe_total = jnp.maximum(total, 1e-30)
    shares = (weighted / safe_total[..., None]).reshape(all_items, query_width)
    level = jnp.where(total > 0, peak + jnp.log(safe_total), NEG)
    first = lax.reduce_precision(level, 8, 7)
    second = lax.reduce_precision(level - first, 8, 7)
    third = level - first - second
    packed = jnp.concatenate([shares, first, second, third], 1).astype(jnp.bfloat16)
    parts = gather(packed).astype(jnp.float32)
    levels = parts[..., query_width:].reshape(pool_size, all_items, 3, group_size)
    levels = levels[:, :, 0] + levels[:, :, 1] + levels[:, :, 2]
    factor = jnp.exp(levels - jnp.max(levels, 0))
    factor = factor / jnp.sum(factor, 0)
    shares = parts[..., :query_width].reshape(pool_size, all_items, group_size, HD)
    attended = jnp.sum(shares * factor[..., None], 0).astype(jnp.bfloat16)
    attended = attended.reshape(prompts, local_heads * query_width)

    attn_out = heads_sum(jnp.dot(attended, out_weight, preferred_element_type=jnp.float32))
    mid_state = (hidden_cols.astype(jnp.float32) + attn_out).astype(jnp.bfloat16)
    whole_state = gather(mid_state).transpose(1, 0, 2).reshape(prompts, width).astype(jnp.float32)
    inverse = lax.rsqrt(jnp.mean(jnp.square(whole_state), -1, keepdims=True) + EPS)
    normed_state = (whole_state * inverse).astype(jnp.bfloat16)
    gate_values = jnp.dot(normed_state, gate_weight, preferred_element_type=jnp.float32)
    up_values = jnp.dot(normed_state, up_weight, preferred_element_type=jnp.float32)
    active = (jax.nn.silu(gate_values) * up_values).astype(jnp.bfloat16)
    partial_out = jnp.dot(active, down_weight, preferred_element_type=jnp.float32).astype(jnp.bfloat16)
    pieces = exchange(partial_out.reshape(prompts, pool_size, block_cols).transpose(1, 0, 2))
    mlp_cols = heads_sum(jnp.sum(pieces.astype(jnp.float32), 0))
    return (mid_state.astype(jnp.float32) + mlp_cols).astype(jnp.bfloat16)


def solution(mesh):
    in_specs = (
        P("groups", None),
        P("groups", "heads", "pool", None),
        P("groups", "heads", "pool", None),
        P(None, "groups", "pool"),
        P(None, "groups"),
        P("groups"),
        P("pool", "heads"),
        P("pool", "heads"),
        P("pool", "heads"),
        P("heads", "pool"),
        P(None, ("pool", "heads")),
        P(None, ("pool", "heads")),
        P(("pool", "heads"), None),
    )
    out_specs = P("groups", "pool")
    return jax.shard_map(per_device, mesh=mesh, in_specs=in_specs, out_specs=out_specs, check_vma=False)
```

time: 358 us -> 180 us (0.50)
  waiting for transfers between devices: 110 us -> 9.97 us
  other arithmetic: 81.8 us -> 47.3 us
  blocking collectives: 82.9 us -> 54.6 us
  between operations: 13.3 us -> 0.32 us
    all_gather x2 -> x0, blocking collectives: 61.7 us -> none  [the longest x1 31.1 us: per_device(): whole_state = lax.all_gather(mid_state, 'pool', axis=1, tiled=True)]
    reduce_scatter x1 -> x0, waiting for transfers between devices: 60 us -> none  [per_device(): lax.psum_scatter(partial_out, 'pool', scatter_dimension=1, tiled=True)]
    all_to_all x0 -> x3, blocking collectives: none -> 54.6 us  [exchange(): return lax.all_to_all(pieces, 'pool', 0, 0, tiled=True)]
    cos x1 -> x0, other arithmetic: 42.2 us -> none  [angle_tables(): return (jnp.cos(angles), jnp.sin(angles))]
    psum x3 -> x0, waiting for transfers between devices: 35.2 us -> none  [the longest x1 18.8 us: per_device(): mlp_cols = lax.psum(mlp_cols, 'heads')]
    psum x1 -> x0, blocking collectives: 21.3 us -> none  [per_device(): lax.psum(jnp.sum(jnp.square(mid_state.astype(jnp.float32)), -1), 'pool')]
    select_n x1 -> x3, other arithmetic: 0.01 us -> 11.5 us  [the longest x2 11.5 us: sin_cos(): cos_out = jnp.where(turns + 1 & 2 == 2, -cos_out, cos_out)]
    all_to_all x3 -> x2, waiting for transfers between devices: 14.6 us -> 7.47 us  [exchange(): return lax.all_to_all(pieces, 'pool', 0, 0, tiled=True)]
  transfers between devices with their start and end apart: 7 -> 4, of which waited for: 6 -> 3; matrix products, arithmetic and copies ran while one was open for 23% -> 24% of each run, Pallas kernels for 0% -> 0%
where the time goes in v1:
time: 180 us; the launch traced here: 179 us
  blocking collectives  54.6 us (30%)
  matrix products  47.6 us (26%)
  other arithmetic  47.3 us (26%)
  starting transfers between devices  13.3 us (7%)
  waiting for transfers between devices  9.97 us (6%)
  local copies, waits for them, and re-layouts  6.06 us (3%)
    all_to_all x3, blocking collectives, exchange(): return lax.all_to_all(pieces, 'pool', 0, 0, tiled=True)  54.6 us
    another operation x4, other arithmetic  19.3 us
    all_to_all x2, starting transfers between devices, exchange(): return lax.all_to_all(pieces, 'pool', 0, 0, tiled=True)  13.3 us
    dot_general x1, matrix products, per_device(): jnp.dot(active, down_weight, preferred_element_type=jnp.float32)  13.2 us
    select_n x2, other arithmetic, sin_cos(): cos_out = jnp.where(turns + 1 & 2 == 2, -cos_out, cos_out)  11.5 us
    convert_element_type x1, other arithmetic, per_device(): key_cache.astype(jnp.float32)  11.3 us
    dot_general x1, matrix products, per_device(): jnp.dot(normed_state, gate_weight, preferred_element_type=jnp.float32)  9.35 us
    dot_general x1, matrix products, per_device(): jnp.einsum('igd,isd->igs', queries, rotated, preferred_element_type=jnp.f...  8.37 us
  transfers between devices with their start and end apart: 4, of which 3 were waited for; matrix products, arithmetic and copies ran while one was open for 24% of the time, Pallas kernels for 0%

profile of v1, /device:TPU:0, one launch (start us, length us, event | category | flops | bytes accessed | tf_op | source)
XLA Modules:
  0.0 179.1 jit_solution(3802055710667244731)
XLA Ops:
  0.0 0.0 copy-start
  0.0 1.2 multiply_reduce_fusion
  1.2 0.1 copy-done
  1.3 1.0 fusion.46
  2.3 1.5 fusion.48
  3.9 4.6 %fusion.50 = f32[16,4096]{1,0:T(8,128)S(1)} fusion(bf16[1024,4096]{1,0:T(8,128)(2,1)} %param.19, f32[16]{0:T(128)S(1)} %add_rsqrt_fusion.1, bf16[16,8192]{1,0:T(8,128)(2,1)} %param.13, s32[]{:T(128)S(6)} %select_n.150), kind=kOutput, calls=%fused_computation.122 | convolution fusion | flops 134266880 | bytes 8683588 | tf_op jit(solution)/shard_map/dot_general | solution.py:114
  8.5 0.1 concatenate.41
  8.6 0.8 pad_maximum_fusion
  9.4 7.3 %all-to-all-start = ((f32[8,8,1280]{2,1,0:T(8,128)}), f32[8,8,1280]{2,1,0:T(8,128)S(1)}, u32[]{:S(2)}, u32[]{:S(2)}) async-start(f32[8,8,1280]{2,1,0:T(8,128)} %pad_maximum_fusion), calls=%async_computation | async-start | bytes 655360 | tf_op jit(solution)/shard_map/all_to_all | solution.py:64
  16.7 0.0 copy-start.2
  16.7 11.3 %convert_element_type.153 = f32[16,4,512,128]{3,2,1,0:T(8,128)} convert(bf16[16,4,512,128]{3,2,1,0:T(8,128)(2,1)} %param.14) | non-fusion elementwise | flops 4194304 | bytes 25165824 | tf_op jit(solution)/shard_map/convert_element_type | solution.py:122
  28.0 0.0 copy-done.2
  28.0 11.4 %negate_select_fusion.1 = (f32[16,512,64]{2,1,0:T(8,128)S(1)}, f32[16,512,64]{2,1,0:T(8,128)S(1)}) fusion(f32[64]{0:T(128)S(1)} %multiply_exponential_fusion, s32[16,512]{1,0:T(8,128)S(1)} %get-tuple-element.18, s32[16,512]{1,0:T(8,128)S(1)} %get-tuple-element.19, s32[16,512]{1,0:T(8,128)S(1)} %get-tuple-element.17, pred[64]{0:T(512)(128)(4,1)S(1)} %get-tuple-element.28, ...), kind=kLoop, calls=%fused_computation.9 | loop fusion | flops 23068672 | bytes 4292992 | tf_op jit(solution)/shard_map/jit(_where)/select_n | solution.py:31
  39.5 0.0 copy-start.3
  39.5 0.0 copy-start.4
  39.5 19.2 %subtract_convert_fusion = (bf16[16,4,512,64]{3,2,1,0:T(8,128)(2,1)}, bf16[16,4,512,64]{3,2,1,0:T(8,128)(2,1)}) fusion(f32[16,4,512,128]{3,2,1,0:T(8,128)} %convert_element_type.153, f32[16,512,64]{2,1,0:T(8,128)S(1)} %get-tuple-element.16, f32[16,512,64]{2,1,0:T(8,128)S(1)} %get-tuple-element.15), kind=kLoop, calls=%fused_computation.2 | loop fusion | flops 16777216 | bytes 29360128 | tf_op jit(solution)/shard_map/convert.11
  58.7 0.0 copy-done.3
  58.7 0.1 copy.41
  58.8 0.0 copy-done.4
  58.8 0.1 broadcast_in_dim.141
  58.9 0.1 lt.47
  59.0 0.6 gather_fusion
  59.5 0.2 slice_reduce_fusion.2
  59.7 0.1 negate_select_fusion.3
  59.8 0.0 all-to-all-done
  59.9 0.1 subtract_convert_fusion.1
  60.0 0.1 pad_maximum_fusion.1
  60.0 0.7 broadcast_in_dim.151
  60.7 6.0 %all-to-all-start.1 = ((bf16[8,8,10,128]{3,1,2,0:T(8,128)(2,1)}), bf16[8,8,10,128]{3,1,2,0:T(8,128)(2,1)S(1)}, u32[]{:S(2)}, u32[]{:S(2)}) async-start(bf16[8,8,10,128]{3,1,2,0:T(8,128)(2,1)} %broadcast_in_dim.151), calls=%async_computation.1 | async-start | bytes 327680 | tf_op jit(solution)/shard_map/all_to_all | solution.py:64
  66.7 0.1 broadcast_compare_fusion
  66.8 7.5 %all-to-all-done.1 = bf16[8,8,10,128]{3,1,2,0:T(8,128)(2,1)S(1)} async-done(((bf16[8,8,10,128]{3,1,2,0:T(8,128)(2,1)}), bf16[8,8,10,128]{3,1,2,0:T(8,128)(2,1)S(1)}, u32[]{:S(2)}, u32[]{:S(2)}) %all-to-all-start.1) | async-done | bytes 163872 | tf_op jit(solution)/shard_map/all_to_all | solution.py:64
  74.3 0.2 fusion.22
  74.6 8.4 %fusion.54 = (f32[64,8]{1,0:T(8,128)S(1)}, f32[64,8,512]{2,1,0:T(8,128)S(1)}) fusion(bf16[64,512,64]{2,1,0:T(8,128)(2,1)} %bitcast.64, bf16[64,512,64]{2,1,0:T(8,128)(2,1)} %bitcast.63, bf16[64,10,128]{2,1,0:T(8,128)(2,1)S(1)} %bitcast.72, pred[64,512]{1,0:T(8,128)(4,1)S(1)} %broadcast_compare_fusion), kind=kOutput, calls=%fused_computation.125 | convolution fusion | flops 84672000 | bytes 9603072 | tf_op jit(solution)/shard_map/igd,isd->igs/dot_general | solution.py:137
  82.9 0.1 copy.43
  83.0 0.1 copy.56
  83.1 0.1 copy.44
  83.2 0.4 fusion.17
  83.6 0.1 copy.46
  83.7 0.1 copy.45
  83.7 0.1 copy.47
  83.8 4.7 %fusion.15 = bf16[64,8,128]{2,1,0:T(8,128)(2,1)S(1)} fusion(bf16[64,512,128]{2,1,0:T(8,128)(2,1)} %bitcast.65, f32[64,8,512]{2,1,0:T(8,128)S(1)} %get-tuple-element.27, f32[64,8]{1,0:T(8,128)S(1)} %copy.44, pred[64,512]{1,0:T(8,128)(4,1)S(1)} %broadcast_compare_fusion, f32[64,8]{1,0:T(8,128)S(1)} %copy.47, f32[64,128]{1,0:T(8,128)S(1)} %bitcast.77, ...), kind=kOutput, calls=%fused_computation.28 | convolution fusion | flops 67895296 | bytes 9639936 | tf_op jit(solution)/shard_map/igs,isd->igd/dot_general | solution.py:147
  88.6 0.1 copy.48
  88.7 0.1 copy.49
  88.8 0.1 copy.50
  88.9 0.1 concatenate.51
  89.0 0.1 broadcast_in_dim.164
  89.1 30.4 %all_to_all.25 = bf16[8,64,1048]{2,1,0:T(8,128)(2,1)} all-to-all(bf16[8,64,1048]{2,1,0:T(8,128)(2,1)S(1)} %broadcast_in_dim.164), channel_id=1, replica_groups=mesh['groups'=2,'pool'=8,'heads'=2] {'pool'}, dimensions={0} | all-to-all | bytes 2146304 | tf_op jit(solution)/shard_map/all_to_all | solution.py:64
  119.5 2.9 %copy.51 = bf16[8,64,1048]{1,2,0:T(8,128)(2,1)S(1)} copy(bf16[8,64,1048]{2,1,0:T(8,128)(2,1)} %all_to_all.25) | data formatting | bytes 2146304 | tf_op jit(solution)/shard_map/all_to_all | solution.py:64
  122.3 0.3 convert_element_type.157
  122.7 0.4 fusion.6
  123.1 0.1 copy.52
  123.3 0.1 convert_element_type.159
  123.4 4.6 %fusion.55 = f32[16,1024]{1,0:T(8,128)S(1)} fusion(bf16[16,4096]{1,0:T(8,128)(2,1)S(1)} %convert_element_type.159, bf16[4096,1024]{1,0:T(8,128)(2,1)} %param.22), kind=kOutput, calls=%fused_computation.126 | convolution fusion | flops 134217728 | bytes 8585216 | tf_op jit(solution)/shard_map/dot_general | solution.py:165
  127.9 0.0 collective-permute-start
  127.9 1.3 collective-permute-done
  129.2 0.8 fusion.26
  130.0 12.2 %all_to_all.26 = bf16[8,16,1024]{2,1,0:T(8,128)(2,1)S(1)} all-to-all(bf16[8,16,1024]{2,1,0:T(8,128)(2,1)S(1)} %broadcast_in_dim.165), channel_id=1, replica_groups=mesh['groups'=2,'pool'=8,'heads'=2] {'pool'}, dimensions={0} | all-to-all | bytes 524288 | tf_op jit(solution)/shard_map/all_to_all | solution.py:64
  142.3 0.2 fusion.18
  142.5 9.3 %fusion.52 = f32[16,928]{1,0:T(8,128)S(1)} fusion(bf16[8192,928]{0,1:T(8,128)(2,1)} %param.23, f32[16,8192]{1,0:T(8,128)S(1)} %bitcast.66, f32[16]{0:T(128)S(1)} %add_rsqrt_fusion), kind=kOutput, calls=%fused_computation.123 | convolution fusion | flops 243531776 | bytes 15788096 | tf_op jit(solution)/shard_map/dot_general | solution.py:170
  151.9 13.2 %convolution_convert_fusion = bf16[16,8192]{1,0:T(8,128)(2,1)S(1)} fusion(bf16[928,8192]{1,0:T(8,128)(2,1)} %param.25, bf16[8192,928]{0,1:T(8,128)(2,1)} %param.24, f32[16,928]{1,0:T(8,128)S(1)} %fusion.52, f32[16,8192]{1,0:T(8,128)S(1)} %bitcast.67, f32[16]{0:T(128)S(1)} %add_rsqrt_fusion), kind=kOutput, calls=%fused_computation.3 | convolution fusion | flops 487021568 | bytes 31254592 | tf_op jit(solution)/shard_map/dot_general | solution.py:173
  165.2 12.0 %all_to_all.27 = bf16[8,16,1024]{2,1,0:T(8,128)(2,1)S(1)} all-to-all(bf16[8,16,1024]{2,1,0:T(8,128)(2,1)S(1)} %bitcast.69), channel_id=1, replica_groups=mesh['groups'=2,'pool'=8,'heads'=2] {'pool'}, dimensions={0} | all-to-all | bytes 524288 | tf_op jit(solution)/shard_map/all_to_all | solution.py:64
  177.2 0.1 collective-permute-start.1
  177.2 1.2 collective-permute-done.1
  178.5 0.6 add_convert_fusion.1
  (30 shorter events, 0.5 us)
Async XLA Ops:
  0.0 1.3 copy-start
  9.4 50.4 %all-to-all-start = ((f32[8,8,1280]{2,1,0:T(8,128)}), f32[8,8,1280]{2,1,0:T(8,128)S(1)}, u32[]{:S(2)}, u32[]{:S(2)}) async-start(f32[8,8,1280]{2,1,0:T(8,128)} %pad_maximum_fusion), calls=%async_computation | async-start | bytes 655360 | tf_op jit(solution)/shard_map/all_to_all | solution.py:64
  16.7 11.3 %copy-start.2 = (s32[3,16,512]{2,1,0:T(8,128)S(1)}, s32[3,16,512]{2,1,0:T(8,128)}, u32[]{:S(2)}) copy-start(s32[3,16,512]{2,1,0:T(8,128)} %param.16) | copy-start | bytes 294916
  39.5 19.2 %copy-start.3 = (s32[3,16]{1,0:T(4,128)S(1)}, s32[3,16]{1,0:T(4,128)}, u32[]{:S(2)}) copy-start(s32[3,16]{1,0:T(4,128)} %param.17) | copy-start | bytes 580
  39.5 19.3 %copy-start.4 = (s32[16]{0:T(128)S(1)}, s32[16]{0:T(128)}, u32[]{:S(2)}) copy-start(s32[16]{0:T(128)} %param.18) | copy-start | bytes 196
  60.7 13.6 %all-to-all-start.1 = ((bf16[8,8,10,128]{3,1,2,0:T(8,128)(2,1)}), bf16[8,8,10,128]{3,1,2,0:T(8,128)(2,1)S(1)}, u32[]{:S(2)}, u32[]{:S(2)}) async-start(bf16[8,8,10,128]{3,1,2,0:T(8,128)(2,1)} %broadcast_in_dim.151), calls=%async_computation.1 | async-start | bytes 327680 | tf_op jit(solution)/shard_map/all_to_all | solution.py:64
  127.9 1.3 collective-permute-start
  151.9 27.2 %copy-start.1 = (bf16[1024,512]{1,0:T(8,128)(2,1)S(1)}, bf16[1024,512]{1,0:T(8,128)(2,1)}, u32[]{:S(2)}) copy-start(bf16[1024,512]{1,0:T(8,128)(2,1)} %param.21) | copy-start | bytes 3145732
  177.2 1.3 collective-permute-start.1

commit v2 on v1

v2 whole, which is shorter than its diff:
```python
import math

import jax
import jax.numpy as jnp
from jax import lax
from jax.experimental import pallas as pl
from jax.experimental.pallas import tpu as pltpu
from jax.sharding import PartitionSpec as P

HD = 128
EPS = 1e-06
THETA = 1000000.0
NEG = -1e30


def sin_cos(angles):
    turns = (angles * (2.0 / math.pi) + 0.5).astype(jnp.int32)
    count = turns.astype(jnp.float32)
    rest = angles - count * 1.5703125
    rest = rest - count * 4.837512969970703125e-4
    rest = rest - count * 7.54978995489188216e-8
    square = rest * rest
    sine = ((-1.9515295891e-4 * square + 8.3321608736e-3) * square - 1.6666654611e-1) * square * rest + rest
    cosine = (
        ((2.443315711809948e-5 * square - 1.388731625493765e-3) * square + 4.166664568298827e-2) * square * square
        - 0.5 * square
        + 1.0
    )
    odd = (turns & 1) == 1
    sin_out = jnp.where(odd, cosine, sine)
    cos_out = jnp.where(odd, sine, cosine)
    sin_out = jnp.where((turns & 2) == 2, -sin_out, sin_out)
    cos_out = jnp.where(((turns + 1) & 2) == 2, -cos_out, cos_out)
    return sin_out, cos_out


def frequencies():
    column = jnp.arange(HD // 2)
    return jnp.exp(column.astype(jnp.float32) * (-2.0 * math.log(THETA) / HD))


def sections():
    first_end = HD // 8
    second_end = first_end + 3 * HD // 16
    column = jnp.arange(HD // 2)
    return (column >= first_end).astype(jnp.int32) + (column >= second_end).astype(jnp.int32)


def small_grant(mebibytes):
    return pltpu.CompilerParams(vmem_limit_bytes=mebibytes << 20)


def rope_keys(key_cache, positions):
    prompts, heads, slots, _ = key_cache.shape
    pairs = prompts // 2
    low_bits = 64
    halves = positions.reshape(3, 2, pairs, slots)
    digits = jnp.stack([halves // low_bits, halves % low_bits], 1)
    digits = jnp.pad(digits.transpose(3, 2, 1, 0, 4).reshape(pairs, 2, 6, slots), ((0, 0), (0, 0), (0, 2), (0, 0)))
    digits = digits.reshape(pairs, 16, slots).astype(jnp.bfloat16)
    one_hot = (sections()[None, :] == jnp.arange(3)[:, None]).astype(jnp.float32)
    one_hot = jnp.concatenate([one_hot * low_bits, one_hot, jnp.zeros((2, HD // 2))], 0)
    blank = jnp.zeros_like(one_hot)
    picker = jnp.concatenate(
        [jnp.concatenate([one_hot, blank], 1), jnp.concatenate([blank, one_hot], 1)], 0
    ).astype(jnp.bfloat16)
    inverse = jnp.tile(frequencies(), 2)[None]
    chunk = min(slots, 64)

    def body(digits_ref, picker_ref, inverse_ref, key_ref, out_ref, *table_refs):
        chosen = lax.dot_general(
            digits_ref[0], picker_ref[...], (((0,), (0,)), ((), ())), preferred_element_type=jnp.float32
        )
        first = lax.broadcasted_iota(jnp.int32, (chunk, HD), 1) < HD // 2
        for start in range(0, slots, chunk):
            rows = slice(start, start + chunk)
            sine, cosine = sin_cos(chosen[rows] * inverse_ref[...])
            cosine_rolled = pltpu.roll(cosine, HD // 2, 1)
            sine_rolled = pltpu.roll(sine, HD // 2, 1)
            table_refs[0][0, rows, :] = jnp.where(first, cosine, cosine_rolled)
            table_refs[0][1, rows, :] = jnp.where(first, cosine_rolled, cosine)
            table_refs[1][0, rows, :] = jnp.where(first, -sine, sine_rolled)
            table_refs[1][1, rows, :] = jnp.where(first, -sine_rolled, sine)
        for half in range(2):
            for start in range(0, slots, chunk):
                rows = slice(start, start + chunk)
                cos_rows = table_refs[0][half, rows, :]
                sin_rows = table_refs[1][half, rows, :]
                for head in range(heads):
                    keys = key_ref[half, 0, head, rows, :].astype(jnp.float32)
                    turned = keys * cos_rows + pltpu.roll(keys, HD // 2, 1) * sin_rows
                    out_ref[half, 0, head, rows, :] = turned.astype(jnp.bfloat16)

    shape = (2, pairs, heads, slots, HD)
    block = pl.BlockSpec((2, 1, heads, slots, HD), lambda i: (0, i, 0, 0, 0))
    rotated = pl.pallas_call(
        body,
        grid=(pairs,),
        in_specs=[
            pl.BlockSpec((1, 16, slots), lambda i: (i, 0, 0)),
            pl.BlockSpec((16, HD), lambda i: (0, 0)),
            pl.BlockSpec((1, HD), lambda i: (0, 0)),
            block,
        ],
        out_specs=block,
        out_shape=jax.ShapeDtypeStruct(shape, jnp.bfloat16),
        scratch_shapes=[pltpu.VMEM((2, slots, HD), jnp.float32)] * 2,
        compiler_params=small_grant(60),
        name="rope_keys",
    )(digits, picker, inverse, key_cache.reshape(shape))
    return rotated.reshape(prompts * heads, slots, HD)


def finish_rows(received, cos_rows, sin_rows):
    pool_size, rows, _ = received.shape

    def body(received_ref, cos_ref, sin_ref, out_ref):
        total = received_ref[0]
        for source in range(1, pool_size):
            total = total + received_ref[source]
        turned = total * cos_ref[...] + pltpu.roll(total, HD // 2, 1) * sin_ref[...]
        turned = turned.astype(jnp.bfloat16)
        for target in range(pool_size):
            out_ref[target] = turned

    return pl.pallas_call(
        body, out_shape=jax.ShapeDtypeStruct((pool_size, rows, HD), jnp.bfloat16), name="finish_rows",
        compiler_params=small_grant(4),
    )(received, cos_rows, sin_rows)


def attend(info, new_rows, rotated, values, local_heads, group_size):
    pool_size = new_rows.shape[0]
    all_items, slots, _ = rotated.shape
    my_count = all_items // pool_size
    pair = 2 if my_count % 2 == 0 else 1
    rows = pair * group_size
    query_rows = my_count * group_size
    scale = HD ** (-0.5)
    prompts = all_items // local_heads

    groups = [[first + k for k in range(pair)] for first in range(0, my_count, pair)]

    def body(info_ref, new_ref, key_ref, value_ref, out_ref):
        block = pl.program_id(0)
        row_index = lax.broadcasted_iota(jnp.int32, (rows, 1), 0)
        slot_index = lax.broadcasted_iota(jnp.int32, (query_rows, slots), 1)
        lane = lax.broadcasted_iota(jnp.int32, (rows, HD), 1)
        holds_own = info_ref[prompts] == 0
        in_item = [row_index // group_size == k for k in range(pair)]

        def spread(piece, width):
            return jnp.concatenate(
                [jnp.broadcast_to(piece(item), (group_size, width)) for item in range(my_count)], 0
            )

        queries = new_ref[0, :query_rows, :].astype(jnp.float32)
        own_rows = new_ref[0, query_rows:, :].astype(jnp.float32)
        scores = []
        for index, items in enumerate(groups):
            part = queries[index * rows : (index + 1) * rows]
            wide_queries = jnp.concatenate([jnp.where(mask, part, 0.0).astype(jnp.bfloat16) for mask in in_item], 1)
            wide_keys = jnp.concatenate([key_ref[item] for item in items], 1)
            scores.append(
                lax.dot_general(
                    wide_queries, wide_keys, (((1,), (1,)), ((), ())), preferred_element_type=jnp.float32
                )
            )
        scores = jnp.concatenate(scores, 0) * scale
        limits = spread(lambda item: jnp.full((1, 1), info_ref[(block * my_count + item) // local_heads]), 1)
        valid = slot_index < limits
        scores = jnp.where(valid, scores, NEG)
        own_keys = spread(lambda item: own_rows[item : item + 1], HD)
        own_values = spread(lambda item: own_rows[my_count + item : my_count + item + 1], HD)
        own_score = jnp.sum(queries * own_keys, 1, keepdims=True) * scale
        own_score = jnp.where(holds_own, own_score, NEG)
        peak = jnp.maximum(jnp.max(scores, 1, keepdims=True), own_score)
        weights = jnp.where(valid, jnp.exp(scores - peak), 0.0)
        own_weight = jnp.where(holds_own, jnp.exp(own_score - peak), 0.0)
        total = jnp.sum(weights, 1, keepdims=True) + own_weight
        coarse = weights.astype(jnp.bfloat16)
        fine = (weights - coarse.astype(jnp.float32)).astype(jnp.bfloat16)
        blended = []
        for index, items in enumerate(groups):
            span = slice(index * rows, (index + 1) * rows)
            wide_values = jnp.concatenate([value_ref[item] for item in items], 1)
            both = jnp.dot(
                jnp.concatenate([coarse[span], fine[span]], 0), wide_values, preferred_element_type=jnp.float32
            )
            both = both[:rows] + both[rows:]
            chosen = both[:, :HD]
            for k in range(1, pair):
                chosen = jnp.where(in_item[k], both[:, k * HD : (k + 1) * HD], chosen)
            blended.append(chosen)
        blended = jnp.concatenate(blended, 0) + own_weight * own_values
        safe_total = jnp.maximum(total, 1e-30)
        out_ref[0, :query_rows, :] = (blended / safe_total).astype(jnp.bfloat16)
        level = jnp.where(total > 0, peak + jnp.log(safe_total), NEG)
        stamp = jnp.zeros((rows, HD), jnp.float32)
        for part in range(3):
            rounded = level.astype(jnp.bfloat16).astype(jnp.float32)
            level = level - rounded
            for index in range(len(groups)):
                stamp = jnp.where(lane == index * 3 + part, rounded[index * rows : (index + 1) * rows], stamp)
        out_ref[0, query_rows:, :] = stamp.astype(jnp.bfloat16)

    cache_block = pl.BlockSpec((my_count, slots, HD), lambda i, info: (i, 0, 0))
    return pl.pallas_call(
        body,
        grid_spec=pltpu.PrefetchScalarGridSpec(
            num_scalar_prefetch=1,
            grid=(pool_size,),
            in_specs=[
                pl.BlockSpec((1,) + new_rows.shape[1:], lambda i, info: (i, 0, 0)),
                cache_block,
                cache_block,
            ],
            out_specs=pl.BlockSpec((1, query_rows + rows, HD), lambda i, info: (i, 0, 0)),
        ),
        out_shape=jax.ShapeDtypeStruct((pool_size, query_rows + rows, HD), jnp.bfloat16),
        name="attend",
        compiler_params=small_grant(60),
    )(info, new_rows, rotated, values)


def combine(parts, my_count, group_size):
    pool_size = parts.shape[0]
    pair = 2 if my_count % 2 == 0 else 1
    rows = pair * group_size
    query_rows = my_count * group_size

    def body(parts_ref, out_ref):
        lane = lax.broadcasted_iota(jnp.int32, (rows, HD), 1)
        stamps = [parts_ref[source, query_rows:, :].astype(jnp.float32) for source in range(pool_size)]
        for group in range(my_count // pair):
            in_group = (lane >= group * 3) & (lane < group * 3 + 3)
            levels = [jnp.sum(jnp.where(in_group, stamp, 0.0), 1, keepdims=True) for stamp in stamps]
            top = levels[0]
            for level in levels[1:]:
                top = jnp.maximum(top, level)
            factors = [jnp.exp(level - top) for level in levels]
            whole = factors[0]
            for factor in factors[1:]:
                whole = whole + factor
            span = slice(group * rows, (group + 1) * rows)
            blended = jnp.zeros((rows, HD), jnp.float32)
            for source in range(pool_size):
                blended = blended + parts_ref[source, span, :].astype(jnp.float32) * factors[source]
            blended = (blended / whole).astype(jnp.bfloat16)
            for target in range(pool_size):
                out_ref[target, span, :] = blended

    return pl.pallas_call(
        body, out_shape=jax.ShapeDtypeStruct((pool_size, query_rows, HD), jnp.bfloat16), name="combine",
        compiler_params=small_grant(4),
    )(parts)


def feed_forward(state, gate_weight, up_weight, down_weight):
    pool_size, prompts, block_cols = state.shape
    width = pool_size * block_cols
    hidden = gate_weight.shape[1]
    across = (((1,), (1,)), ((), ()))

    def body(state_ref, gate_hbm, up_hbm, down_hbm, out_ref, gate_ref, up_ref, down_ref, sems):
        spans = [slice(k * block_cols, (k + 1) * block_cols) for k in range(pool_size)]
        copies = []
        for index, span in enumerate(spans):
            for which, (source, target) in enumerate(((gate_hbm, gate_ref), (up_hbm, up_ref), (down_hbm, down_ref))):
                copies.append(pltpu.make_async_copy(source.at[:, span], target.at[:, span], sems.at[which, index]))
        for index in range(pool_size):
            copies[3 * index].start()
            copies[3 * index + 1].start()
        for index in range(pool_size):
            copies[3 * index + 2].start()
        squares = jnp.zeros((prompts, 1), jnp.float32)
        for source in range(pool_size):
            rows = state_ref[source].astype(jnp.float32)
            squares = squares + jnp.sum(rows * rows, 1, keepdims=True)
        inverse = lax.rsqrt(squares / width + EPS)
        gate_values = jnp.zeros((prompts, hidden), jnp.float32)
        up_values = jnp.zeros((prompts, hidden), jnp.float32)
        for index, span in enumerate(spans):
            rows = (state_ref[index].astype(jnp.float32) * inverse).astype(jnp.bfloat16)
            copies[3 * index].wait()
            gate_values = gate_values + lax.dot_general(
                rows, gate_ref[:, span], across, preferred_element_type=jnp.float32
            )
            copies[3 * index + 1].wait()
            up_values = up_values + lax.dot_general(
                rows, up_ref[:, span], across, preferred_element_type=jnp.float32
            )
        active = (gate_values / (1.0 + jnp.exp(-gate_values)) * up_values).astype(jnp.bfloat16)
        for index, span in enumerate(spans):
            copies[3 * index + 2].wait()
            out_ref[index] = jnp.dot(active, down_ref[:, span], preferred_element_type=jnp.float32).astype(
                jnp.bfloat16
            )

    whole = pl.BlockSpec(memory_space=pltpu.VMEM)
    return pl.pallas_call(
        body,
        in_specs=[whole] + [pl.BlockSpec(memory_space=pltpu.HBM)] * 3,
        scratch_shapes=[
            pltpu.VMEM((hidden, width), gate_weight.dtype),
            pltpu.VMEM((hidden, width), up_weight.dtype),
            pltpu.VMEM((hidden, width), down_weight.dtype),
            pltpu.SemaphoreType.DMA((3, pool_size)),
        ],
        out_shape=jax.ShapeDtypeStruct(state.shape, jnp.bfloat16),
        name="feed_forward",
        compiler_params=small_grant(60),
        cost_estimate=pl.CostEstimate(
            flops=6 * prompts * width * hidden, bytes_accessed=6 * width * hidden, transcendentals=prompts * hidden
        ),
    )(state, gate_weight.T, up_weight.T, down_weight)


def exchange(pieces):
    return lax.all_to_all(pieces, "pool", 0, 0, tiled=True)


def gather(block):
    pool_size = lax.axis_size("pool")
    return exchange(jnp.broadcast_to(block[None], (pool_size,) + block.shape))


def heads_sum(values):
    size = lax.axis_size("heads")
    total = values
    moved = values
    for _ in range(size - 1):
        moved = lax.ppermute(moved, "heads", [(k, (k + 1) % size) for k in range(size)])
        total = total + moved
    return total


def per_device(
    hidden_in,
    key_cache,
    value_cache,
    positions,
    query_pos,
    lengths,
    query_weight,
    key_weight,
    value_weight,
    out_weight,
    gate_weight,
    up_weight,
    down_weight,
):
    pool_index = lax.axis_index("pool")
    pool_size = lax.axis_size("pool")
    prompts, width = hidden_in.shape
    local_heads, seq_local = key_cache.shape[1:3]
    query_width = query_weight.shape[1] // local_heads
    group_size = query_width // HD
    all_items = prompts * local_heads
    my_count = all_items // pool_size
    my_start = pool_index * my_count
    block_cols = width // pool_size

    squares = jnp.sum(jnp.square(hidden_in.astype(jnp.float32)), -1, keepdims=True)
    hidden_cols = lax.dynamic_slice_in_dim(hidden_in, pool_index * block_cols, block_cols, 1)
    normed_cols = (hidden_cols.astype(jnp.float32) * lax.rsqrt(squares / width + EPS)).astype(jnp.bfloat16)
    projected = [
        jnp.dot(normed_cols, weight, preferred_element_type=jnp.float32).reshape(pool_size, -1, HD)
        for weight in (query_weight, key_weight, value_weight)
    ]
    info = jnp.concatenate([lengths - pool_index * seq_local, jnp.full((1,), pool_index, jnp.int32)])
    projected, info = lax.optimization_barrier((jnp.concatenate(projected, 1), info))
    received = exchange(projected)

    rotated = rope_keys(key_cache, positions)
    value_rows = value_cache.reshape(all_items, seq_local, HD)
    row_items = my_start + jnp.concatenate(
        [jnp.repeat(jnp.arange(my_count), group_size), jnp.arange(my_count), jnp.arange(my_count)]
    )
    row_prompts = row_items // local_heads
    turning = (jnp.arange(my_count * (group_size + 2)) < my_count * (group_size + 1))[:, None]
    picked = (row_prompts[:, None] == jnp.arange(prompts)) & turning
    section = sections()
    chosen = jnp.zeros((row_items.shape[0], HD // 2), jnp.int32)
    for axis in range(3):
        ids = jnp.sum(jnp.where(picked, query_pos[axis][None], 0), 1)
        chosen = jnp.where(section == axis, ids[:, None], chosen)
    sine, cosine = sin_cos(chosen.astype(jnp.float32) * frequencies())
    cos_rows = jnp.concatenate([cosine, cosine], 1)
    sin_rows = jnp.concatenate([-sine, sine], 1)
    received, rotated = lax.optimization_barrier((received, rotated))
    new_rows = exchange(finish_rows(received, cos_rows, sin_rows))

    parts = exchange(attend(info, new_rows, rotated, value_rows, local_heads, group_size))
    attended = exchange(combine(parts, my_count, group_size))
    attended = attended.reshape(prompts, local_heads * query_width)

    attn_out = heads_sum(jnp.dot(attended, out_weight, preferred_element_type=jnp.float32))
    mid_state = (hidden_cols.astype(jnp.float32) + attn_out).astype(jnp.bfloat16)
    pieces = exchange(feed_forward(gather(mid_state), gate_weight, up_weight, down_weight))
    mlp_cols = heads_sum(jnp.sum(pieces.astype(jnp.float32), 0))
    return (mid_state.astype(jnp.float32) + mlp_cols).astype(jnp.bfloat16)


def solution(mesh):
    in_specs = (
        P("groups", None),
        P("groups", "heads", "pool", None),
        P("groups", "heads", "pool", None),
        P(None, "groups", "pool"),
        P(None, "groups"),
        P("groups"),
        P("pool", "heads"),
        P("pool", "heads"),
        P("pool", "heads"),
        P("heads", "pool"),
        P(None, ("pool", "heads")),
        P(None, ("pool", "heads")),
        P(("pool", "heads"), None),
    )
    out_specs = P("groups", "pool")
    return jax.shard_map(per_device, mesh=mesh, in_specs=in_specs, out_specs=out_specs, check_vma=False)
```

time: 180 us -> 130 us (0.72)
  other arithmetic: 47.3 us -> 5.43 us
  Pallas kernels: 0 us -> 40.8 us
  matrix products: 47.6 us -> 11.9 us
  waiting for transfers between devices: 9.97 us -> 2.5 us
  starting transfers between devices: 13.3 us -> 7.35 us
  blocking collectives: 54.6 us -> 59.3 us
  local copies, waits for them, and re-layouts: 6.06 us -> 1.76 us
    pallas_call x0 -> x5, Pallas kernels: none -> 40.8 us  [the longest x1 16.5 us: feed_forward(): pl.pallas_call(body, in_specs=[whole] + [pl.BlockSpec(memory_space=pltpu....]
    dot_general x5 -> x0, matrix products: 35.8 us -> none  [the longest x1 13.2 us: per_device(): jnp.dot(active, down_weight, preferred_element_type=jnp.float32)]
    another operation x4 -> x3, other arithmetic: 19.3 us -> 0.19 us
    convert_element_type x2 -> x1, other arithmetic: 11.6 us -> 0.01 us  [rope_keys(): (sections()[None, :] == jnp.arange(3)[:, None]).astype(jnp.float32)]
    select_n x3 -> x1, other arithmetic: 11.5 us -> 0.09 us  [per_device(): row_prompts = row_items // local_heads]
    all_to_all x2 -> x1, waiting for transfers between devices: 7.47 us -> 0.01 us  [exchange(): return lax.all_to_all(pieces, 'pool', 0, 0, tiled=True)]
    all_to_all x2 -> x1, starting transfers between devices: 13.3 us -> 7.28 us  [exchange(): return lax.all_to_all(pieces, 'pool', 0, 0, tiled=True)]
    all_to_all x3 -> x5, blocking collectives: 54.6 us -> 59.3 us  [exchange(): return lax.all_to_all(pieces, 'pool', 0, 0, tiled=True)]
  transfers between devices with their start and end apart: 4 -> 3, of which waited for: 3 -> 2; matrix products, arithmetic and copies ran while one was open for 24% -> 2% of each run, Pallas kernels for 0% -> 10%
where the time goes in v2:
time: 130 us; the launch traced here: 129 us
  blocking collectives  59.3 us (46%)
  Pallas kernels  40.8 us (31%)
  matrix products  11.9 us (9%)
  starting transfers between devices  7.35 us (6%)
  other arithmetic  5.43 us (4%)
  waiting for transfers between devices  2.5 us (2%)
  local copies, waits for them, and re-layouts  1.76 us (1%)
    all_to_all x5, blocking collectives, exchange(): return lax.all_to_all(pieces, 'pool', 0, 0, tiled=True)  59.3 us
    pallas_call x1, Pallas kernels, feed_forward(): pl.pallas_call(body, in_specs=[whole] + [pl.BlockSpec(memory_space=pltpu....  16.5 us
    pallas_call x1, Pallas kernels, rope_keys(): pl.pallas_call(body, grid=(pairs,), in_specs=[pl.BlockSpec((1, 16, slots)...  12.8 us
    pallas_call x1, Pallas kernels, attend(): pl.pallas_call(body, grid_spec=pltpu.PrefetchScalarGridSpec(num_scalar_pr...  11.2 us
    all_to_all x1, starting transfers between devices, exchange(): return lax.all_to_all(pieces, 'pool', 0, 0, tiled=True)  7.28 us
    dot_general x3, matrix products, per_device(): jnp.dot(normed_cols, weight, preferred_element_type=jnp.float32)  7.26 us
    dot_general x1, matrix products, per_device(): jnp.dot(attended, out_weight, preferred_element_type=jnp.float32)  4.61 us
  transfers between devices with their start and end apart: 3, of which 2 were waited for; matrix products, arithmetic and copies ran while one was open for 2% of the time, Pallas kernels for 10%

profile of v2, /device:TPU:0, one launch (start us, length us, event | category | flops | bytes accessed | tf_op | source)
XLA Modules:
  0.0 129.2 jit_solution(7047560208667118500)
XLA Ops:
  0.0 0.0 copy-start
  0.0 1.2 multiply_reduce_fusion
  1.2 0.1 copy-done
  1.3 1.0 fusion.20
  2.3 0.0 copy-start.4
  2.4 1.5 %fusion.18 = f32[16,512]{1,0:T(8,128)S(1)} fusion(bf16[1024,512]{1,0:T(8,128)(2,1)} %param.21, f32[16]{0:T(128)S(1)} %add_rsqrt_fusion, bf16[16,8192]{1,0:T(8,128)(2,1)} %param.13, s32[]{:T(128)S(6)} %select_n.71), kind=kOutput, calls=%fused_computation.72 | convolution fusion | flops 16826368 | bytes 1114180 | tf_op jit(solution)/shard_map/dot_general | solution.py:368
  3.9 0.0 copy-start.3
  3.9 0.0 copy-start.2
  3.9 4.7 %fusion.22 = f32[16,4096]{1,0:T(8,128)S(1)} fusion(bf16[1024,4096]{1,0:T(8,128)(2,1)} %param.19, f32[16]{0:T(128)S(1)} %add_rsqrt_fusion, bf16[16,8192]{1,0:T(8,128)(2,1)} %param.13, s32[]{:T(128)S(6)} %select_n.71), kind=kOutput, calls=%fused_computation.74 | convolution fusion | flops 134266880 | bytes 8683588 | tf_op jit(solution)/shard_map/dot_general | solution.py:368
  8.7 0.0 copy-done.4
  8.7 0.7 pad_add_fusion.info_ref
  9.3 0.8 pad_maximum_fusion
  10.1 7.3 %all-to-all-start = ((f32[8,80,128]{2,1,0:T(8,128)}), f32[8,80,128]{2,1,0:T(8,128)S(1)}, u32[]{:S(2)}, u32[]{:S(2)}) async-start(f32[8,80,128]{2,1,0:T(8,128)} %pad_maximum_fusion), calls=%async_computation | async-start | bytes 655360 | tf_op jit(solution)/shard_map/all_to_all | solution.py:320
  17.5 0.0 copy-done.3
  17.5 0.1 pad.21.clone
  17.6 0.1 maximum_convert_fusion
  17.7 0.7 fusion.13.picker_ref
  18.3 0.0 copy-done.2
  18.3 0.1 fusion
  18.5 0.1 copy.20
  18.5 0.7 pad_bitcast_fusion.digits_ref
  19.2 0.6 broadcast_in_dim_tile.3.inverse_ref
  19.8 0.1 concatenate.40
  19.9 12.8 %rope_keys.1 = bf16[2,8,4,512,128]{4,3,2,1,0:T(8,128)(2,1)} custom-call(bf16[8,16,512]{2,1,0:T(8,128)(2,1)} %pad_bitcast_fusion.digits_ref, bf16[16,128]{1,0:T(8,128)(2,1)} %fusion.13.picker_ref, f32[1,128]{1,0:T(1,128)} %broadcast_in_dim_tile.3.inverse_ref, bf16[2,8,4,512,128]{4,3,2,1,0:T(8,128)(2,1)} %bitcast.53), custom_call_target="tpu_custom_call" | custom-call | tf_op jit(solution)/shard_map/rope_keys/pallas_call | solution.py:96
  32.7 0.1 and_select_fusion
  32.8 0.1 select_reduce_fusion.2
  32.9 0.2 fusion.17
  33.0 0.1 pad_maximum_fusion.2
  33.1 0.0 all-to-all-done.received_ref
  33.1 0.1 finish_rows.1
  33.2 13.5 %all_to_all.30.new_ref = bf16[8,80,128]{2,1,0:T(8,128)(2,1)} all-to-all(bf16[8,80,128]{2,1,0:T(8,128)(2,1)S(1)} %finish_rows.1), channel_id=1, replica_groups=mesh['groups'=2,'pool'=8,'heads'=2] {'pool'}, dimensions={0} | all-to-all | bytes 327680 | tf_op jit(solution)/shard_map/all_to_all | solution.py:320
  46.7 11.2 %attend.1 = bf16[8,80,128]{2,1,0:T(8,128)(2,1)} custom-call(s32[17]{0:T(128)} %pad_add_fusion.info_ref, bf16[8,80,128]{2,1,0:T(8,128)(2,1)} %all_to_all.30.new_ref, bf16[64,512,128]{2,1,0:T(8,128)(2,1)} %bitcast.49, bf16[64,512,128]{2,1,0:T(8,128)(2,1)} %bitcast.52), custom_call_target="tpu_custom_call" | custom-call | tf_op jit(solution)/shard_map/attend/pallas_call | solution.py:208
  57.8 10.9 %all_to_all.31.parts_ref = bf16[8,80,128]{2,1,0:T(8,128)(2,1)S(1)} all-to-all(bf16[8,80,128]{2,1,0:T(8,128)(2,1)} %attend.1), channel_id=1, replica_groups=mesh['groups'=2,'pool'=8,'heads'=2] {'pool'}, dimensions={0} | all-to-all | bytes 327680 | tf_op jit(solution)/shard_map/all_to_all | solution.py:320
  68.7 0.2 combine.1
  68.9 9.7 %all_to_all.32 = bf16[8,64,128]{2,1,0:T(8,128)(2,1)S(1)} all-to-all(bf16[8,64,128]{2,1,0:T(8,128)(2,1)S(1)} %combine.1), channel_id=1, replica_groups=mesh['groups'=2,'pool'=8,'heads'=2] {'pool'}, dimensions={0} | all-to-all | bytes 262144 | tf_op jit(solution)/shard_map/all_to_all | solution.py:320
  78.6 0.1 reshape.204
  78.7 4.6 %fusion.24 = f32[16,1024]{1,0:T(8,128)S(1)} fusion(bf16[16,4096]{1,0:T(8,128)(2,1)S(1)} %reshape.204, bf16[4096,1024]{1,0:T(8,128)(2,1)} %param.22), kind=kOutput, calls=%fused_computation.75 | convolution fusion | flops 134217728 | bytes 8585216 | tf_op jit(solution)/shard_map/dot_general | solution.py:398
  83.3 0.0 collective-permute-start
  83.3 1.3 collective-permute-done
  84.6 0.8 fusion.5
  85.4 12.6 %all_to_all.33.state_ref = bf16[8,16,1024]{2,1,0:T(8,128)(2,1)} all-to-all(bf16[8,16,1024]{2,1,0:T(8,128)(2,1)S(1)} %broadcast_in_dim.104), channel_id=1, replica_groups=mesh['groups'=2,'pool'=8,'heads'=2] {'pool'}, dimensions={0} | all-to-all | bytes 524288 | tf_op jit(solution)/shard_map/all_to_all | solution.py:320
  98.0 0.0 copy-start.1
  98.0 16.5 %feed_forward.1 = bf16[8,16,1024]{2,1,0:T(8,128)(2,1)} custom-call(bf16[8,16,1024]{2,1,0:T(8,128)(2,1)} %all_to_all.33.state_ref, bf16[928,8192]{1,0:T(8,128)(2,1)} %bitcast.50, bf16[928,8192]{1,0:T(8,128)(2,1)} %bitcast.51, bf16[928,8192]{1,0:T(8,128)(2,1)} %down_hbm.1), custom_call_target="tpu_custom_call" | custom-call | flops 729808896 | bytes 45613056 | tf_op jit(solution)/shard_map/feed_forward/pallas_call | solution.py:301
  114.5 12.7 %all_to_all.34 = bf16[8,16,1024]{2,1,0:T(8,128)(2,1)S(1)} all-to-all(bf16[8,16,1024]{2,1,0:T(8,128)(2,1)} %feed_forward.1), channel_id=1, replica_groups=mesh['groups'=2,'pool'=8,'heads'=2] {'pool'}, dimensions={0} | all-to-all | bytes 524288 | tf_op jit(solution)/shard_map/all_to_all | solution.py:320
  127.2 0.1 collective-permute-start.1
  127.3 1.2 collective-permute-done.1
  128.5 0.6 add_convert_fusion
  129.2 0.0 copy-done.1
  (21 shorter events, 0.2 us)
Async XLA Ops:
  0.0 1.3 %copy-start = (bf16[1024,512]{1,0:T(8,128)(2,1)S(1)}, bf16[1024,512]{1,0:T(8,128)(2,1)}, u32[]{:S(2)}) copy-start(bf16[1024,512]{1,0:T(8,128)(2,1)} %param.20) | copy-start | bytes 3145732
  2.3 6.3 %copy-start.4 = (s32[16]{0:T(128)S(1)}, s32[16]{0:T(128)}, u32[]{:S(2)}) copy-start(s32[16]{0:T(128)} %param.18) | copy-start | bytes 196
  3.9 13.6 %copy-start.3 = (s32[3,16]{1,0:T(4,128)S(1)}, s32[3,16]{1,0:T(4,128)}, u32[]{:S(2)}) copy-start(s32[3,16]{1,0:T(4,128)} %param.17) | copy-start | bytes 580
  3.9 14.4 %copy-start.2 = (s32[3,16,512]{2,1,0:T(8,128)S(1)}, s32[3,16,512]{2,1,0:T(8,128)}, u32[]{:S(2)}) copy-start(s32[3,16,512]{2,1,0:T(8,128)} %param.16) | copy-start | bytes 294916
  10.1 23.0 %all-to-all-start = ((f32[8,80,128]{2,1,0:T(8,128)}), f32[8,80,128]{2,1,0:T(8,128)S(1)}, u32[]{:S(2)}, u32[]{:S(2)}) async-start(f32[8,80,128]{2,1,0:T(8,128)} %pad_maximum_fusion), calls=%async_computation | async-start | bytes 655360 | tf_op jit(solution)/shard_map/all_to_all | solution.py:320
  83.3 1.3 collective-permute-start
  98.0 31.2 %copy-start.1 = (bf16[1024,512]{1,0:T(8,128)(2,1)S(1)}, bf16[1024,512]{1,0:T(8,128)(2,1)}, u32[]{:S(2)}) copy-start(bf16[1024,512]{1,0:T(8,128)(2,1)} %param.20) | copy-start | bytes 3145732
  127.2 1.3 %collective-permute-start.1 = (f32[16,1024]{1,0:T(8,128)S(1)}, f32[16,1024]{1,0:T(8,128)S(1)}, u32[]{:S(2)}, u32[]{:S(2)}) collective-permute-start(f32[16,1024]{1,0:T(8,128)S(1)} %convert_reduce_fusion), channel_id=1, source_target_pairs={{0,1},{1,0},{2,3},{3,2},{4,5},{5,4},{6,7},{7,6},{8,9},{9,8},{10,11... | collective-permute-start | bytes 196616 | tf_op jit(solution)/shard_map/ppermute | solution.py:333

commit v3 on v2

--- a/solution.py
+++ b/solution.py
@@ -50,65 +50,217 @@
     return pltpu.CompilerParams(vmem_limit_bytes=mebibytes << 20)
 
 
-def rope_keys(key_cache, positions):
-    prompts, heads, slots, _ = key_cache.shape
-    pairs = prompts // 2
-    low_bits = 64
-    halves = positions.reshape(3, 2, pairs, slots)
-    digits = jnp.stack([halves // low_bits, halves % low_bits], 1)
-    digits = jnp.pad(digits.transpose(3, 2, 1, 0, 4).reshape(pairs, 2, 6, slots), ((0, 0), (0, 0), (0, 2), (0, 0)))
-    digits = digits.reshape(pairs, 16, slots).astype(jnp.bfloat16)
-    one_hot = (sections()[None, :] == jnp.arange(3)[:, None]).astype(jnp.float32)
-    one_hot = jnp.concatenate([one_hot * low_bits, one_hot, jnp.zeros((2, HD // 2))], 0)
-    blank = jnp.zeros_like(one_hot)
-    picker = jnp.concatenate(
-        [jnp.concatenate([one_hot, blank], 1), jnp.concatenate([blank, one_hot], 1)], 0
-    ).astype(jnp.bfloat16)
+def rope_keys(key_cache, positions, first_pair, last_pair, partner):
+    _, pairs, heads, slots, _ = key_cache.shape
+    low_bits = 6
+    chunk = min(slots, 64)
+    count = last_pair - first_pair
     inverse = jnp.tile(frequencies(), 2)[None]
-    chunk = min(slots, 64)
-
-    def body(digits_ref, picker_ref, inverse_ref, key_ref, out_ref, *table_refs):
-        chosen = lax.dot_general(
-            digits_ref[0], picker_ref[...], (((0,), (0,)), ((), ())), preferred_element_type=jnp.float32
-        )
+
+    def body(positions_ref, inverse_ref, key_hbm, *refs):
+        out_hbm, key_ref, out_ref, chosen_ref, cos_ref, sin_ref, sems = refs[-7:]
+
+        def copy_in(index):
+            return pltpu.make_async_copy(key_hbm.at[:, first_pair + index], key_ref.at[:, index], sems.at[0, index])
+
+        def copy_out(index):
+            return pltpu.make_async_copy(out_ref.at[:, index], out_hbm.at[:, first_pair + index], sems.at[1, index])
+
+        for index in range(count):
+            copy_in(index).start()
         first = lax.broadcasted_iota(jnp.int32, (chunk, HD), 1) < HD // 2
-        for start in range(0, slots, chunk):
-            rows = slice(start, start + chunk)
-            sine, cosine = sin_cos(chosen[rows] * inverse_ref[...])
-            cosine_rolled = pltpu.roll(cosine, HD // 2, 1)
-            sine_rolled = pltpu.roll(sine, HD // 2, 1)
-            table_refs[0][0, rows, :] = jnp.where(first, cosine, cosine_rolled)
-            table_refs[0][1, rows, :] = jnp.where(first, cosine_rolled, cosine)
-            table_refs[1][0, rows, :] = jnp.where(first, -sine, sine_rolled)
-            table_refs[1][1, rows, :] = jnp.where(first, -sine_rolled, sine)
-        for half in range(2):
+        row = lax.broadcasted_iota(jnp.int32, (16, HD), 0)
+        lane = lax.broadcasted_iota(jnp.int32, (16, HD), 1)
+        column = lane % (HD // 2)
+        first_end = HD // 8
+        section = (column >= first_end).astype(jnp.int32) + (column >= first_end + 3 * HD // 16).astype(jnp.int32)
+        within = row % 8
+        own_half = row // 8 == lane // (HD // 2)
+        picker = jnp.where(own_half & (within == section), float(1 << low_bits), 0.0)
+        picker = jnp.where(own_half & (within == section + 3), 1.0, picker).astype(jnp.bfloat16)
+        blank = jnp.zeros((2, slots), jnp.float32)
+
+        def step(index, carry):
+            digits = []
+            for half in range(2):
+                ids = [positions_ref[axis, pl.ds(half * pairs + first_pair + index, 1), :] for axis in range(3)]
+                digits += [(value >> low_bits).astype(jnp.float32) for value in ids]
+                digits += [(value & ((1 << low_bits) - 1)).astype(jnp.float32) for value in ids]
+                digits.append(blank)
+            chosen_ref[...] = lax.dot_general(
+                jnp.concatenate(digits, 0).astype(jnp.bfloat16),
+                picker,
+                (((0,), (0,)), ((), ())),
+                preferred_element_type=jnp.float32,
+            )
             for start in range(0, slots, chunk):
                 rows = slice(start, start + chunk)
-                cos_rows = table_refs[0][half, rows, :]
-                sin_rows = table_refs[1][half, rows, :]
-                for head in range(heads):
-                    keys = key_ref[half, 0, head, rows, :].astype(jnp.float32)
-                    turned = keys * cos_rows + pltpu.roll(keys, HD // 2, 1) * sin_rows
-                    out_ref[half, 0, head, rows, :] = turned.astype(jnp.bfloat16)
-
-    shape = (2, pairs, heads, slots, HD)
-    block = pl.BlockSpec((2, 1, heads, slots, HD), lambda i: (0, i, 0, 0, 0))
-    rotated = pl.pallas_call(
+                sine, cosine = sin_cos(chosen_ref[rows, :] * inverse_ref[...])
+                cosine_rolled = pltpu.roll(cosine, HD // 2, 1)
+                sine_rolled = pltpu.roll(sine, HD // 2, 1)
+                cos_ref[0, rows, :] = jnp.where(first, cosine, cosine_rolled)
+                cos_ref[1, rows, :] = jnp.where(first, cosine_rolled, cosine)
+                sin_ref[0, rows, :] = jnp.where(first, -sine, sine_rolled)
+                sin_ref[1, rows, :] = jnp.where(first, -sine_rolled, sine)
+            copy_in(index).wait()
+            for half in range(2):
+                for start in range(0, slots, chunk):
+                    rows = slice(start, start + chunk)
+                    cos_rows = cos_ref[half, rows, :]
+                    sin_rows = sin_ref[half, rows, :]
+                    for head in range(heads):
+                        keys = key_ref[half, index, head, rows, :].astype(jnp.float32)
+                        turned = keys * cos_rows + pltpu.roll(keys, HD // 2, 1) * sin_rows
+                        out_ref[half, index, head, rows, :] = turned.astype(jnp.bfloat16)
+            copy_out(index).start()
+            return carry
+
+        lax.fori_loop(0, count, step, 0)
+        for index in range(count):
+            copy_out(index).wait()
+
+    vmem = pl.BlockSpec(memory_space=pltpu.VMEM)
+    hbm = pl.BlockSpec(memory_space=pltpu.HBM)
+    partners = () if partner is None else (partner,)
+    return pl.pallas_call(
         body,
-        grid=(pairs,),
-        in_specs=[
-            pl.BlockSpec((1, 16, slots), lambda i: (i, 0, 0)),
-            pl.BlockSpec((16, HD), lambda i: (0, 0)),
-            pl.BlockSpec((1, HD), lambda i: (0, 0)),
-            block,
+        in_specs=[vmem, vmem, hbm] + [hbm for _ in partners],
+        out_specs=hbm,
+        out_shape=jax.ShapeDtypeStruct(key_cache.shape, jnp.bfloat16),
+        input_output_aliases={3: 0} if partners else {},
+        scratch_shapes=[
+            pltpu.VMEM((2, count) + key_cache.shape[2:], jnp.bfloat16),
+            pltpu.VMEM((2, count) + key_cache.shape[2:], jnp.bfloat16),
+            pltpu.VMEM((slots, HD), jnp.float32),
+            pltpu.VMEM((2, slots, HD), jnp.float32),
+            pltpu.VMEM((2, slots, HD), jnp.float32),
+            pltpu.SemaphoreType.DMA((2, count)),
         ],
-        out_specs=block,
-        out_shape=jax.ShapeDtypeStruct(shape, jnp.bfloat16),
-        scratch_shapes=[pltpu.VMEM((2, slots, HD), jnp.float32)] * 2,
-        compiler_params=small_grant(60),
+        compiler_params=small_grant(56),
         name="rope_keys",
-    )(digits, picker, inverse, key_cache.reshape(shape))
-    return rotated.reshape(prompts * heads, slots, HD)
+    )(positions, inverse, key_cache, *partners)
+
+
+def project(hidden_in, weights, pool_size, local_heads, group_size):
+    prompts, width = hidden_in.shape
+    block_cols = width // pool_size
+    my_count = prompts * local_heads // pool_size
+    rows = my_count * (group_size + 2)
+    columns = [weight.shape[1] for weight in weights]
+    query_columns = columns[0]
+    pieces = max(1, min(8, query_columns // 512))
+    piece = query_columns // pieces
+
+    def place(kind, head, group):
+        if kind == 0:
+            return lambda item: item * group_size + group
+        return lambda item: my_count * (group_size + kind - 1) + item
+
+    def body(hidden_ref, query_hbm, key_hbm, value_hbm, out_ref, query_ref, key_ref, value_ref, flat_ref, sems):
+        copies = []
+        for index in range(pieces):
+            span = slice(index * piece, (index + 1) * piece)
+            copies.append(pltpu.make_async_copy(query_hbm.at[:, span], query_ref.at[:, span], sems.at[index]))
+        copies.append(pltpu.make_async_copy(key_hbm, key_ref, sems.at[pieces]))
+        copies.append(pltpu.make_async_copy(value_hbm, value_ref, sems.at[pieces + 1]))
+        for copy in copies:
+            copy.start()
+        hidden = hidden_ref[...].astype(jnp.float32)
+        squares = jnp.sum(hidden * hidden, 1, keepdims=True)
+        start = pl.multiple_of(lax.axis_index("pool") * block_cols, block_cols)
+        mine = hidden_ref[:, pl.ds(start, block_cols)].astype(jnp.float32)
+        normed = (mine * lax.rsqrt(squares / width + EPS)).astype(jnp.bfloat16)
+
+        def spread(kind, first_block, count, values):
+            for offset in range(count):
+                flat_ref[offset * prompts : (offset + 1) * prompts, :] = values[:, offset * HD : (offset + 1) * HD]
+                number = first_block + offset
+                head, group = (number // group_size, number % group_size) if kind == 0 else (number, 0)
+                row_of = place(kind, head, group)
+                if my_count >= local_heads:
+                    per_device = my_count // local_heads
+                    for turn in range(per_device):
+                        out_ref[pl.ds(row_of(turn * local_heads + head), pool_size, stride=rows), :] = flat_ref[
+                            pl.ds(offset * prompts + turn, pool_size, stride=per_device), :
+                        ]
+                else:
+                    split = local_heads // my_count
+                    base = (head // my_count) * rows + row_of(head % my_count)
+                    out_ref[pl.ds(base, prompts, stride=split * rows), :] = flat_ref[
+                        offset * prompts : (offset + 1) * prompts, :
+                    ]
+
+        for index in range(pieces):
+            span = slice(index * piece, (index + 1) * piece)
+            copies[index].wait()
+            values = jnp.dot(normed, query_ref[:, span], preferred_element_type=jnp.float32)
+            spread(0, index * (piece // HD), piece // HD, values)
+        for kind, ref in ((1, key_ref), (2, value_ref)):
+            copies[pieces + kind - 1].wait()
+            values = jnp.dot(normed, ref[...], preferred_element_type=jnp.float32)
+            spread(kind, 0, local_heads, values)
+
+    vmem = pl.BlockSpec(memory_space=pltpu.VMEM)
+    hbm = pl.BlockSpec(memory_space=pltpu.HBM)
+    out = pl.pallas_call(
+        body,
+        in_specs=[vmem, hbm, hbm, hbm],
+        out_specs=vmem,
+        out_shape=jax.ShapeDtypeStruct((pool_size * rows, HD), jnp.float32),
+        scratch_shapes=[pltpu.VMEM(weight.shape, weight.dtype) for weight in weights]
+        + [
+            pltpu.VMEM((prompts * max(piece // HD, local_heads), HD), jnp.float32),
+            pltpu.SemaphoreType.DMA((pieces + 2,)),
+        ],
+        compiler_params=small_grant(56),
+        name="project",
+    )(hidden_in, *weights)
+    return out.reshape(pool_size, rows, HD)
+
+
+def project_out(attended, out_weight, prompts):
+    total_rows = attended.shape[0] * attended.shape[1]
+    blocks = total_rows // prompts
+    attended = attended.reshape(total_rows, HD)
+    pieces = max(1, min(8, blocks // 2))
+    per_piece = blocks // pieces
+    depth = per_piece * HD
+
+    def body(attended_ref, weight_hbm, out_ref, weight_ref, wide_ref, sems):
+        copies = []
+        for index in range(pieces):
+            span = slice(index * depth, (index + 1) * depth)
+            copies.append(pltpu.make_async_copy(weight_hbm.at[span], weight_ref.at[span], sems.at[index]))
+            copies[-1].start()
+        wide_ref[...] = attended_ref[...].astype(jnp.float32)
+        total = jnp.zeros(out_ref.shape, jnp.float32)
+        for index in range(pieces):
+            rows = [
+                wide_ref[pl.ds(index * per_piece + k, prompts, stride=blocks), :].astype(jnp.bfloat16)
+                for k in range(per_piece)
+            ]
+            copies[index].wait()
+            total = total + jnp.dot(
+                jnp.concatenate(rows, 1),
+                weight_ref[index * depth : (index + 1) * depth, :],
+                preferred_element_type=jnp.float32,
+            )
+        out_ref[...] = total
+
+    vmem = pl.BlockSpec(memory_space=pltpu.VMEM)
+    return pl.pallas_call(
+        body,
+        in_specs=[vmem, pl.BlockSpec(memory_space=pltpu.HBM)],
+        out_specs=vmem,
+        out_shape=jax.ShapeDtypeStruct((prompts, out_weight.shape[1]), jnp.float32),
+        scratch_shapes=[
+            pltpu.VMEM(out_weight.shape, out_weight.dtype),
+            pltpu.VMEM((total_rows, HD), jnp.float32),
+            pltpu.SemaphoreType.DMA((pieces,)),
+        ],
+        compiler_params=small_grant(53),
+        name="project_out",
+    )(attended, out_weight)
 
 
 def finish_rows(received, cos_rows, sin_rows):
@@ -129,7 +281,7 @@
     )(received, cos_rows, sin_rows)
 
 
-def attend(info, new_rows, rotated, values, local_heads, group_size):
+def attend(lengths, new_rows, rotated, values, local_heads, group_size):
     pool_size = new_rows.shape[0]
     all_items, slots, _ = rotated.shape
     my_count = all_items // pool_size
@@ -137,16 +289,35 @@
     rows = pair * group_size
     query_rows = my_count * group_size
     scale = HD ** (-0.5)
-    prompts = all_items // local_heads
 
     groups = [[first + k for k in range(pair)] for first in range(0, my_count, pair)]
 
-    def body(info_ref, new_ref, key_ref, value_ref, out_ref):
-        block = pl.program_id(0)
+    def body(lengths_ref, new_ref, key_hbm, value_hbm, out_ref, key_refs, value_refs, sems):
+        def copies(block):
+            span = pl.ds(block * my_count, my_count)
+            return (
+                pltpu.make_async_copy(key_hbm.at[span], key_refs.at[block], sems.at[0, block]),
+                pltpu.make_async_copy(value_hbm.at[span], value_refs.at[block], sems.at[1, block]),
+            )
+
+        for block in range(pool_size):
+            for copy in copies(block):
+                copy.start()
+        pool_index = lax.axis_index("pool")
+
+        def step(block, carry):
+            one_block(
+                block, pool_index, copies(block), lengths_ref, new_ref, key_refs.at[block], value_refs.at[block], out_ref
+            )
+            return carry
+
+        lax.fori_loop(0, pool_size, step, 0)
+
+    def one_block(block, pool_index, copies, lengths_ref, new_ref, key_ref, value_ref, out_ref):
         row_index = lax.broadcasted_iota(jnp.int32, (rows, 1), 0)
         slot_index = lax.broadcasted_iota(jnp.int32, (query_rows, slots), 1)
         lane = lax.broadcasted_iota(jnp.int32, (rows, HD), 1)
-        holds_own = info_ref[prompts] == 0
+        holds_own = pool_index == 0
         in_item = [row_index // group_size == k for k in range(pair)]
 
         def spread(piece, width):
@@ -154,8 +325,10 @@
                 [jnp.broadcast_to(piece(item), (group_size, width)) for item in range(my_count)], 0
             )
 
-        queries = new_ref[0, :query_rows, :].astype(jnp.float32)
-        own_rows = new_ref[0, query_rows:, :].astype(jnp.float32)
+        queries = new_ref[block, :query_rows, :].astype(jnp.float32)
+        own_rows = new_ref[block, query_rows:, :].astype(jnp.float32)
+        for copy in copies:
+            copy.wait()
         scores = []
         for index, items in enumerate(groups):
             part = queries[index * rows : (index + 1) * rows]
@@ -167,8 +340,8 @@
                 )
             )
         scores = jnp.concatenate(scores, 0) * scale
-        limits = spread(lambda item: jnp.full((1, 1), info_ref[(block * my_count + item) // local_heads]), 1)
-        valid = slot_index < limits
+        limits = spread(lambda item: jnp.full((1, 1), lengths_ref[(block * my_count + item) // local_heads]), 1)
+        valid = slot_index + pool_index * slots < limits
         scores = jnp.where(valid, scores, NEG)
         own_keys = spread(lambda item: own_rows[item : item + 1], HD)
         own_values = spread(lambda item: own_rows[my_count + item : my_count + item + 1], HD)
@@ -194,7 +367,7 @@
             blended.append(chosen)
         blended = jnp.concatenate(blended, 0) + own_weight * own_values
         safe_total = jnp.maximum(total, 1e-30)
-        out_ref[0, :query_rows, :] = (blended / safe_total).astype(jnp.bfloat16)
+        out_ref[block, :query_rows, :] = (blended / safe_total).astype(jnp.bfloat16)
         level = jnp.where(total > 0, peak + jnp.log(safe_total), NEG)
         stamp = jnp.zeros((rows, HD), jnp.float32)
         for part in range(3):
@@ -202,25 +375,24 @@
             level = level - rounded
             for index in range(len(groups)):
                 stamp = jnp.where(lane == index * 3 + part, rounded[index * rows : (index + 1) * rows], stamp)
-        out_ref[0, query_rows:, :] = stamp.astype(jnp.bfloat16)
-
-    cache_block = pl.BlockSpec((my_count, slots, HD), lambda i, info: (i, 0, 0))
+        out_ref[block, query_rows:, :] = stamp.astype(jnp.bfloat16)
+
+    vmem = pl.BlockSpec(memory_space=pltpu.VMEM)
+    hbm = pl.BlockSpec(memory_space=pltpu.HBM)
+    cache_shape = (pool_size, my_count, slots, HD)
     return pl.pallas_call(
         body,
-        grid_spec=pltpu.PrefetchScalarGridSpec(
-            num_scalar_prefetch=1,
-            grid=(pool_size,),
-            in_specs=[
-                pl.BlockSpec((1,) + new_rows.shape[1:], lambda i, info: (i, 0, 0)),
-                cache_block,
-                cache_block,
-            ],
-            out_specs=pl.BlockSpec((1, query_rows + rows, HD), lambda i, info: (i, 0, 0)),
-        ),
+        in_specs=[pl.BlockSpec(memory_space=pltpu.SMEM), vmem, hbm, hbm],
+        out_specs=vmem,
         out_shape=jax.ShapeDtypeStruct((pool_size, query_rows + rows, HD), jnp.bfloat16),
+        scratch_shapes=[
+            pltpu.VMEM(cache_shape, rotated.dtype),
+            pltpu.VMEM(cache_shape, values.dtype),
+            pltpu.SemaphoreType.DMA((2, pool_size)),
+        ],
+        compiler_params=small_grant(53),
         name="attend",
-        compiler_params=small_grant(60),
-    )(info, new_rows, rotated, values)
+    )(lengths, new_rows, rotated, values)
 
 
 def combine(parts, my_count, group_size):
@@ -309,7 +481,7 @@
         ],
         out_shape=jax.ShapeDtypeStruct(state.shape, jnp.bfloat16),
         name="feed_forward",
-        compiler_params=small_grant(60),
+        compiler_params=small_grant(48),
         cost_estimate=pl.CostEstimate(
             flops=6 * prompts * width * hidden, bytes_accessed=6 * width * hidden, transcendentals=prompts * hidden
         ),
@@ -361,18 +533,13 @@
     my_start = pool_index * my_count
     block_cols = width // pool_size
 
-    squares = jnp.sum(jnp.square(hidden_in.astype(jnp.float32)), -1, keepdims=True)
-    hidden_cols = lax.dynamic_slice_in_dim(hidden_in, pool_index * block_cols, block_cols, 1)
-    normed_cols = (hidden_cols.astype(jnp.float32) * lax.rsqrt(squares / width + EPS)).astype(jnp.bfloat16)
-    projected = [
-        jnp.dot(normed_cols, weight, preferred_element_type=jnp.float32).reshape(pool_size, -1, HD)
-        for weight in (query_weight, key_weight, value_weight)
-    ]
-    info = jnp.concatenate([lengths - pool_index * seq_local, jnp.full((1,), pool_index, jnp.int32)])
-    projected, info = lax.optimization_barrier((jnp.concatenate(projected, 1), info))
-    received = exchange(projected)
-
-    rotated = rope_keys(key_cache, positions)
+    weights = (query_weight, key_weight, value_weight)
+    received = exchange(project(hidden_in, weights, pool_size, local_heads, group_size))
+
+    pairs = prompts // 2
+    early = (5 * pairs) // 8
+    paired_keys = key_cache.reshape((2, pairs) + key_cache.shape[1:])
+    rotated = rope_keys(paired_keys, positions, 0, early, None)
     value_rows = value_cache.reshape(all_items, seq_local, HD)
     row_items = my_start + jnp.concatenate(
         [jnp.repeat(jnp.arange(my_count), group_size), jnp.arange(my_count), jnp.arange(my_count)]
@@ -389,13 +556,14 @@
     cos_rows = jnp.concatenate([cosine, cosine], 1)
     sin_rows = jnp.concatenate([-sine, sine], 1)
     received, rotated = lax.optimization_barrier((received, rotated))
-    new_rows = exchange(finish_rows(received, cos_rows, sin_rows))
-
-    parts = exchange(attend(info, new_rows, rotated, value_rows, local_heads, group_size))
+    finished, rotated = lax.optimization_barrier((finish_rows(received, cos_rows, sin_rows), rotated))
+    new_rows = exchange(finished)
+    rotated = rope_keys(paired_keys, positions, early, pairs, rotated).reshape(all_items, seq_local, HD)
+
+    parts = exchange(attend(lengths, new_rows, rotated, value_rows, local_heads, group_size))
     attended = exchange(combine(parts, my_count, group_size))
-    attended = attended.reshape(prompts, local_heads * query_width)
-
-    attn_out = heads_sum(jnp.dot(attended, out_weight, preferred_element_type=jnp.float32))
+    attn_out = heads_sum(project_out(attended, out_weight, prompts))
+    hidden_cols = lax.dynamic_slice_in_dim(hidden_in, pool_index * block_cols, block_cols, 1)
     mid_state = (hidden_cols.astype(jnp.float32) + attn_out).astype(jnp.bfloat16)
     pieces = exchange(feed_forward(gather(mid_state), gate_weight, up_weight, down_weight))
     mlp_cols = heads_sum(jnp.sum(pieces.astype(jnp.float32), 0))

time: 130 us -> 113 us (0.87)
  blocking collectives: 59.3 us -> 45.7 us
  matrix products: 11.9 us -> 0 us
  Pallas kernels: 40.8 us -> 46.6 us
  starting transfers between devices: 7.35 us -> 12.3 us
  other arithmetic: 5.43 us -> 1.89 us
  waiting for transfers between devices: 2.5 us -> 5.48 us
    all_to_all x5 -> x4, blocking collectives: 59.3 us -> 45.7 us  [exchange(): return lax.all_to_all(pieces, 'pool', 0, 0, tiled=True)]
    dot_general x4 -> x0, matrix products: 11.9 us -> none  [the longest x3 7.26 us: per_device(): jnp.dot(normed_cols, weight, preferred_element_type=jnp.float32)]
    pallas_call x2 -> x5, Pallas kernels: 23.9 us -> 30.8 us  [the longest x2 13.6 us: rope_keys(): pl.pallas_call(body, in_specs=[vmem, vmem, hbm] + [hbm for _ in partners]...]
    all_to_all x1 -> x2, starting transfers between devices: 7.28 us -> 12.1 us  [exchange(): return lax.all_to_all(pieces, 'pool', 0, 0, tiled=True)]
    all_to_all x1 -> x2, waiting for transfers between devices: 0.01 us -> 3 us  [exchange(): return lax.all_to_all(pieces, 'pool', 0, 0, tiled=True)]
    concatenate x3 -> x0, other arithmetic: 2.1 us -> none  [the longest x1 0.78 us: per_device(): jnp.concatenate(projected, 1)]
    pallas_call x1, Pallas kernels: 16.5 us -> 14.8 us  [feed_forward(): pl.pallas_call(body, in_specs=[whole] + [pl.BlockSpec(memory_space=pltpu....]
  transfers between devices with their start and end apart: 3 -> 4, of which waited for: 2 -> 4; matrix products, arithmetic and copies ran while one was open for 2% -> 1% of each run, Pallas kernels for 10% -> 12%
where the time goes in v3:
time: 113 us
  Pallas kernels  46.6 us (41%)
  blocking collectives  45.7 us (40%)
  starting transfers between devices  12.3 us (11%)
  waiting for transfers between devices  5.48 us (5%)
  other arithmetic  1.89 us (2%)
    all_to_all x4, blocking collectives, exchange(): return lax.all_to_all(pieces, 'pool', 0, 0, tiled=True)  45.7 us
    pallas_call x1, Pallas kernels, feed_forward(): pl.pallas_call(body, in_specs=[whole] + [pl.BlockSpec(memory_space=pltpu....  14.8 us
    pallas_call x2, Pallas kernels, rope_keys(): pl.pallas_call(body, in_specs=[vmem, vmem, hbm] + [hbm for _ in partners]...  13.6 us
    all_to_all x2, starting transfers between devices, exchange(): return lax.all_to_all(pieces, 'pool', 0, 0, tiled=True)  12.1 us
    pallas_call x1, Pallas kernels, attend(): pl.pallas_call(body, in_specs=[pl.BlockSpec(memory_space=pltpu.SMEM), vme...  7.28 us
    pallas_call x1, Pallas kernels, project(): pl.pallas_call(body, in_specs=[vmem, hbm, hbm, hbm], out_specs=vmem, out_...  6.14 us
    pallas_call x1, Pallas kernels, project_out(): pl.pallas_call(body, in_specs=[vmem, pl.BlockSpec(memory_space=pltpu.HBM)...  3.74 us
    all_to_all x2, waiting for transfers between devices, exchange(): return lax.all_to_all(pieces, 'pool', 0, 0, tiled=True)  3 us
  transfers between devices with their start and end apart: 4, of which 4 were waited for; matrix products, arithmetic and copies ran while one was open for 1% of the time, Pallas kernels for 12%

profile of v3, /device:TPU:0, one launch (start us, length us, event | category | flops | bytes accessed | tf_op | source)
XLA Modules:
  0.0 112.8 jit_solution(16896598962182149945)
XLA Ops:
  0.0 0.0 copy-start.1
  0.0 6.1 %project.1 = f32[640,128]{1,0:T(8,128)} custom-call(bf16[16,8192]{1,0:T(8,128)(2,1)} %hidden_ref.1, bf16[1024,4096]{1,0:T(8,128)(2,1)} %query_hbm.1, bf16[1024,512]{1,0:T(8,128)(2,1)} %key_hbm.1, bf16[1024,512]{1,0:T(8,128)(2,1)} %value_hbm.1), custom_call_target="tpu_custom_call" | custom-call | tf_op jit(solution)/shard_map/project/pallas_call | solution.py:205
  6.1 7.3 %all-to-all-start = ((f32[8,80,128]{2,1,0:T(8,128)}), f32[8,80,128]{2,1,0:T(8,128)S(1)}, u32[]{:S(2)}, u32[]{:S(2)}) async-start(f32[8,80,128]{2,1,0:T(8,128)} %bitcast.20), calls=%async_computation | async-start | bytes 655360 | tf_op jit(solution)/shard_map/all_to_all | solution.py:492
  13.5 0.0 copy-done.1
  13.5 0.6 broadcast_in_dim_tile.6.inverse_ref
  14.1 0.1 concatenate.15
  14.2 7.9 %rope_keys.2.refs_0_ = bf16[2,8,4,512,128]{4,3,2,1,0:T(8,128)(2,1)} custom-call(s32[3,16,512]{2,1,0:T(8,128)} %positions_ref.3, f32[1,128]{1,0:T(1,128)} %broadcast_in_dim_tile.6.inverse_ref, bf16[2,8,4,512,128]{4,3,2,1,0:T(8,128)(2,1)} %bitcast.15), custom_call_target="tpu_custom_call" | custom-call | tf_op jit(solution)/shard_map/rope_keys/pallas_call | solution.py:125
  22.1 0.1 and_select_fusion
  22.2 0.1 select_reduce_fusion.2
  22.3 0.2 fusion.5
  22.5 0.1 pad_maximum_fusion
  22.6 1.2 %all-to-all-done.received_ref = f32[8,80,128]{2,1,0:T(8,128)S(1)} async-done(((f32[8,80,128]{2,1,0:T(8,128)}), f32[8,80,128]{2,1,0:T(8,128)S(1)}, u32[]{:S(2)}, u32[]{:S(2)}) %all-to-all-start) | async-done | bytes 327712 | tf_op jit(solution)/shard_map/all_to_all | solution.py:492
  23.7 0.8 finish_rows.1
  24.5 4.8 %all-to-all-start.1 = ((bf16[8,80,128]{2,1,0:T(8,128)(2,1)}), bf16[8,80,128]{2,1,0:T(8,128)(2,1)S(1)}, u32[]{:S(2)}, u32[]{:S(2)}) async-start(bf16[8,80,128]{2,1,0:T(8,128)(2,1)} %finish_rows.1), calls=%async_computation.1 | async-start | bytes 327680 | tf_op jit(solution)/shard_map/all_to_all | solution.py:492
  29.3 0.0 copy-start
  29.3 5.7 %rope_keys.3 = bf16[2,8,4,512,128]{4,3,2,1,0:T(8,128)(2,1)} custom-call(s32[3,16,512]{2,1,0:T(8,128)} %positions_ref.3, f32[1,128]{1,0:T(1,128)} %broadcast_in_dim_tile.6.inverse_ref, bf16[2,8,4,512,128]{4,3,2,1,0:T(8,128)(2,1)} %bitcast.16, bf16[2,8,4,512,128]{4,3,2,1,0:T(8,128)(2,1)} %rope_keys.2.refs_0_), custom_call_target="tpu_custom_call", output_to_operand_aliasing={{}: (3, {})} | custom-call | tf_op jit(solution)/shard_map/rope_keys/pallas_call | solution.py:125
  35.1 1.8 %all-to-all-done.1.new_ref = bf16[8,80,128]{2,1,0:T(8,128)(2,1)S(1)} async-done(((bf16[8,80,128]{2,1,0:T(8,128)(2,1)}), bf16[8,80,128]{2,1,0:T(8,128)(2,1)S(1)}, u32[]{:S(2)}, u32[]{:S(2)}) %all-to-all-start.1) | async-done | bytes 163872 | tf_op jit(solution)/shard_map/all_to_all | solution.py:492
  36.9 0.0 copy-done
  36.9 7.3 %attend.1 = bf16[8,80,128]{2,1,0:T(8,128)(2,1)S(1)} custom-call(s32[16]{0:T(128)S(1)} %copy-done, bf16[8,80,128]{2,1,0:T(8,128)(2,1)S(1)} %all-to-all-done.1.new_ref, bf16[64,512,128]{2,1,0:T(8,128)(2,1)} %bitcast.14, bf16[64,512,128]{2,1,0:T(8,128)(2,1)} %bitcast.19), custom_call_target="tpu_custom_call" | custom-call | tf_op jit(solution)/shard_map/attend/pallas_call | solution.py:383
  44.2 11.6 %all_to_all.30.parts_ref = bf16[8,80,128]{2,1,0:T(8,128)(2,1)S(1)} all-to-all(bf16[8,80,128]{2,1,0:T(8,128)(2,1)S(1)} %attend.1), channel_id=1, replica_groups=mesh['groups'=2,'pool'=8,'heads'=2] {'pool'}, dimensions={0} | all-to-all | bytes 327680 | tf_op jit(solution)/shard_map/all_to_all | solution.py:492
  55.7 0.2 combine.1
  56.0 9.7 %all_to_all.31 = bf16[8,64,128]{2,1,0:T(8,128)(2,1)S(1)} all-to-all(bf16[8,64,128]{2,1,0:T(8,128)(2,1)S(1)} %combine.1), channel_id=1, replica_groups=mesh['groups'=2,'pool'=8,'heads'=2] {'pool'}, dimensions={0} | all-to-all | bytes 262144 | tf_op jit(solution)/shard_map/all_to_all | solution.py:492
  65.7 3.7 %project_out.1 = f32[16,1024]{1,0:T(8,128)S(1)} custom-call(bf16[512,128]{1,0:T(8,128)(2,1)S(1)} %bitcast.13, bf16[4096,1024]{1,0:T(8,128)(2,1)} %weight_hbm.1), custom_call_target="tpu_custom_call" | custom-call | tf_op jit(solution)/shard_map/project_out/pallas_call | solution.py:251
  69.4 0.1 collective-permute-start
  69.5 1.2 %collective-permute-done = f32[16,1024]{1,0:T(8,128)S(1)} collective-permute-done((f32[16,1024]{1,0:T(8,128)S(1)}, f32[16,1024]{1,0:T(8,128)S(1)}, u32[]{:S(2)}, u32[]{:S(2)}) %collective-permute-start) | collective-permute-done | bytes 65568 | tf_op jit(solution)/shard_map/ppermute | solution.py:505
  70.8 0.8 add_convert_fusion.1
  71.6 11.9 %all_to_all.32.state_ref = bf16[8,16,1024]{2,1,0:T(8,128)(2,1)S(1)} all-to-all(bf16[8,16,1024]{2,1,0:T(8,128)(2,1)S(1)} %broadcast_in_dim.92), channel_id=1, replica_groups=mesh['groups'=2,'pool'=8,'heads'=2] {'pool'}, dimensions={0} | all-to-all | bytes 524288 | tf_op jit(solution)/shard_map/all_to_all | solution.py:492
  83.5 14.8 %feed_forward.1 = bf16[8,16,1024]{2,1,0:T(8,128)(2,1)S(1)} custom-call(bf16[8,16,1024]{2,1,0:T(8,128)(2,1)S(1)} %all_to_all.32.state_ref, bf16[928,8192]{1,0:T(8,128)(2,1)} %bitcast.17, bf16[928,8192]{1,0:T(8,128)(2,1)} %bitcast.18, bf16[928,8192]{1,0:T(8,128)(2,1)} %down_hbm.1), custom_call_target="tpu_custom_call" | custom-call | flops 729808896 | bytes 45613056 | tf_op jit(solution)/shard_map/feed_forward/pallas_call | solution.py:473
  98.3 12.5 %all_to_all.33 = bf16[8,16,1024]{2,1,0:T(8,128)(2,1)S(1)} all-to-all(bf16[8,16,1024]{2,1,0:T(8,128)(2,1)S(1)} %feed_forward.1), channel_id=1, replica_groups=mesh['groups'=2,'pool'=8,'heads'=2] {'pool'}, dimensions={0} | all-to-all | bytes 524288 | tf_op jit(solution)/shard_map/all_to_all | solution.py:492
  110.8 0.1 collective-permute-start.1
  110.9 1.2 %collective-permute-done.1 = f32[16,1024]{1,0:T(8,128)S(1)} collective-permute-done((f32[16,1024]{1,0:T(8,128)S(1)}, f32[16,1024]{1,0:T(8,128)S(1)}, u32[]{:S(2)}, u32[]{:S(2)}) %collective-permute-start.1) | collective-permute-done | bytes 65568 | tf_op jit(solution)/shard_map/ppermute | solution.py:505
  112.1 0.6 add_convert_fusion
  (11 shorter events, 0.1 us)
Async XLA Ops:
  0.0 13.5 %copy-start.1 = (s32[3,16]{1,0:T(4,128)S(1)}, s32[3,16]{1,0:T(4,128)}, u32[]{:S(2)}) copy-start(s32[3,16]{1,0:T(4,128)} %param.17) | copy-start | bytes 580
  6.1 17.6 %all-to-all-start = ((f32[8,80,128]{2,1,0:T(8,128)}), f32[8,80,128]{2,1,0:T(8,128)S(1)}, u32[]{:S(2)}, u32[]{:S(2)}) async-start(f32[8,80,128]{2,1,0:T(8,128)} %bitcast.20), calls=%async_computation | async-start | bytes 655360 | tf_op jit(solution)/shard_map/all_to_all | solution.py:492
  24.5 12.4 %all-to-all-start.1 = ((bf16[8,80,128]{2,1,0:T(8,128)(2,1)}), bf16[8,80,128]{2,1,0:T(8,128)(2,1)S(1)}, u32[]{:S(2)}, u32[]{:S(2)}) async-start(bf16[8,80,128]{2,1,0:T(8,128)(2,1)} %finish_rows.1), calls=%async_computation.1 | async-start | bytes 327680 | tf_op jit(solution)/shard_map/all_to_all | solution.py:492
  29.3 7.6 %copy-start = (s32[16]{0:T(128)S(1)}, s32[16]{0:T(128)}, u32[]{:S(2)}) copy-start(s32[16]{0:T(128)} %lengths_ref.1) | copy-start | bytes 196
  69.4 1.3 %collective-permute-start = (f32[16,1024]{1,0:T(8,128)S(1)}, f32[16,1024]{1,0:T(8,128)S(1)}, u32[]{:S(2)}, u32[]{:S(2)}) collective-permute-start(f32[16,1024]{1,0:T(8,128)S(1)} %project_out.1), channel_id=1, source_target_pairs={{0,1},{1,0},{2,3},{3,2},{4,5},{5,4},{6,7},{7,6},{8,9},{9,8},{10,11... | collective-permute-start | bytes 196616 | tf_op jit(solution)/shard_map/ppermute | solution.py:505
  110.8 1.3 %collective-permute-start.1 = (f32[16,1024]{1,0:T(8,128)S(1)}, f32[16,1024]{1,0:T(8,128)S(1)}, u32[]{:S(2)}, u32[]{:S(2)}) collective-permute-start(f32[16,1024]{1,0:T(8,128)S(1)} %convert_reduce_fusion), channel_id=1, source_target_pairs={{0,1},{1,0},{2,3},{3,2},{4,5},{5,4},{6,7},{7,6},{8,9},{9,8},{10,11... | collective-permute-start | bytes 196616 | tf_op jit(solution)/shard_map/ppermute | solution.py:505

commit v4 on v3

--- a/solution.py
+++ b/solution.py
@@ -21,11 +21,8 @@
     rest = rest - count * 7.54978995489188216e-8
     square = rest * rest
     sine = ((-1.9515295891e-4 * square + 8.3321608736e-3) * square - 1.6666654611e-1) * square * rest + rest
-    cosine = (
-        ((2.443315711809948e-5 * square - 1.388731625493765e-3) * square + 4.166664568298827e-2) * square * square
-        - 0.5 * square
-        + 1.0
-    )
+    cosine = ((2.443315711809948e-5 * square - 1.388731625493765e-3) * square + 4.166664568298827e-2) * square
+    cosine = (cosine - 0.5) * square + 1.0
     odd = (turns & 1) == 1
     sin_out = jnp.where(odd, cosine, sine)
     cos_out = jnp.where(odd, sine, cosine)
@@ -44,6 +41,10 @@
     second_end = first_end + 3 * HD // 16
     column = jnp.arange(HD // 2)
     return (column >= first_end).astype(jnp.int32) + (column >= second_end).astype(jnp.int32)
+
+
+def in_hbm(array):
+    return pltpu.with_memory_space_constraint(array, pltpu.HBM)
 
 
 def small_grant(mebibytes):
@@ -156,7 +157,9 @@
             return lambda item: item * group_size + group
         return lambda item: my_count * (group_size + kind - 1) + item
 
-    def body(hidden_ref, query_hbm, key_hbm, value_hbm, out_ref, query_ref, key_ref, value_ref, flat_ref, sems):
+    def body(hidden_hbm, query_hbm, key_hbm, value_hbm, out_ref, query_ref, key_ref, value_ref, flat_ref, hidden_ref, sems):
+        hidden_copy = pltpu.make_async_copy(hidden_hbm, hidden_ref, sems.at[pieces + 2])
+        hidden_copy.start()
         copies = []
         for index in range(pieces):
             span = slice(index * piece, (index + 1) * piece)
@@ -165,6 +168,7 @@
         copies.append(pltpu.make_async_copy(value_hbm, value_ref, sems.at[pieces + 1]))
         for copy in copies:
             copy.start()
+        hidden_copy.wait()
         hidden = hidden_ref[...].astype(jnp.float32)
         squares = jnp.sum(hidden * hidden, 1, keepdims=True)
         start = pl.multiple_of(lax.axis_index("pool") * block_cols, block_cols)
@@ -204,17 +208,18 @@
     hbm = pl.BlockSpec(memory_space=pltpu.HBM)
     out = pl.pallas_call(
         body,
-        in_specs=[vmem, hbm, hbm, hbm],
+        in_specs=[hbm, hbm, hbm, hbm],
         out_specs=vmem,
         out_shape=jax.ShapeDtypeStruct((pool_size * rows, HD), jnp.float32),
         scratch_shapes=[pltpu.VMEM(weight.shape, weight.dtype) for weight in weights]
         + [
             pltpu.VMEM((prompts * max(piece // HD, local_heads), HD), jnp.float32),
-            pltpu.SemaphoreType.DMA((pieces + 2,)),
+            pltpu.VMEM(hidden_in.shape, hidden_in.dtype),
+            pltpu.SemaphoreType.DMA((pieces + 3,)),
         ],
         compiler_params=small_grant(56),
         name="project",
-    )(hidden_in, *weights)
+    )(in_hbm(hidden_in), *[in_hbm(weight) for weight in weights])
     return out.reshape(pool_size, rows, HD)
 
 
@@ -428,64 +433,110 @@
     )(parts)
 
 
-def feed_forward(state, gate_weight, up_weight, down_weight):
-    pool_size, prompts, block_cols = state.shape
+def gather_by_halves(block):
+    pool_size = lax.axis_size("pool")
+
+    def device(pool, core):
+        return 2 * pool + core
+
+    parts = []
+    for turn in range(pool_size // 2):
+        pairs = []
+        for pool in range(pool_size):
+            target = (pool + 2 * turn) % pool_size
+            if turn:
+                pairs.append((device(pool, 0), device(target, 0)))
+            pairs.append((device(pool, 1), device(target ^ 1, 1)))
+        parts.append(lax.ppermute(block, ("pool", "heads"), pairs))
+    parts[0] = jnp.where(lax.axis_index("heads") == 0, block, parts[0])
+    mine = jnp.stack(parts)
+    return mine, lax.ppermute(mine, "heads", [(0, 1), (1, 0)])
+
+
+def sources_by_halves(pool_size):
+    pool = lax.axis_index("pool")
+    core = lax.axis_index("heads")
+    straight = [(pool + pool_size - 2 * turn) % pool_size for turn in range(pool_size // 2)]
+    other = pool + 1 - 2 * (pool % 2)
+    crossed = [(other + pool_size - 2 * turn) % pool_size for turn in range(pool_size // 2)]
+    mine = [jnp.where(core == 0, a, b) for a, b in zip(straight, crossed)]
+    theirs = [jnp.where(core == 0, b, a) for a, b in zip(straight, crossed)]
+    return mine + theirs
+
+
+def feed_forward(states, gate_weight, up_weight, down_weight, pool_size):
+    _, prompts, block_cols = states[0].shape
     width = pool_size * block_cols
-    hidden = gate_weight.shape[1]
+    hidden = gate_weight.shape[0]
     across = (((1,), (1,)), ((), ()))
 
-    def body(state_ref, gate_hbm, up_hbm, down_hbm, out_ref, gate_ref, up_ref, down_ref, sems):
-        spans = [slice(k * block_cols, (k + 1) * block_cols) for k in range(pool_size)]
+    def body(*refs):
+        state_refs = refs[: len(states)]
+        gate_hbm, up_hbm, down_hbm, out_ref, gate_ref, up_ref, down_ref, sems = refs[len(states) :]
+        sources = list(range(pool_size)) if len(states) == 1 else sources_by_halves(pool_size)
+        blocks = [(ref, index) for ref in state_refs for index in range(ref.shape[0])]
         copies = []
-        for index, span in enumerate(spans):
-            for which, (source, target) in enumerate(((gate_hbm, gate_ref), (up_hbm, up_ref), (down_hbm, down_ref))):
-                copies.append(pltpu.make_async_copy(source.at[:, span], target.at[:, span], sems.at[which, index]))
+        spans = []
+        for turn, source in enumerate(sources):
+            start = source * block_cols
+            if len(states) > 1:
+                start = pl.multiple_of(start, block_cols)
+            spans.append(pl.ds(start, block_cols))
+            for which, (origin, held) in enumerate(((gate_hbm, gate_ref), (up_hbm, up_ref))):
+                copies.append(
+                    pltpu.make_async_copy(origin.at[:, spans[-1]], held.at[:, spans[-1]], sems.at[which, turn])
+                )
+                copies[-1].start()
+        down_copies = []
         for index in range(pool_size):
-            copies[3 * index].start()
-            copies[3 * index + 1].start()
-        for index in range(pool_size):
-            copies[3 * index + 2].start()
+            span = slice(index * block_cols, (index + 1) * block_cols)
+            down_copies.append(pltpu.make_async_copy(down_hbm.at[:, span], down_ref.at[:, span], sems.at[2, index]))
+            down_copies[-1].start()
         squares = jnp.zeros((prompts, 1), jnp.float32)
-        for source in range(pool_size):
-            rows = state_ref[source].astype(jnp.float32)
+        for ref, index in blocks:
+            rows = ref[index].astype(jnp.float32)
             squares = squares + jnp.sum(rows * rows, 1, keepdims=True)
         inverse = lax.rsqrt(squares / width + EPS)
         gate_values = jnp.zeros((prompts, hidden), jnp.float32)
         up_values = jnp.zeros((prompts, hidden), jnp.float32)
-        for index, span in enumerate(spans):
-            rows = (state_ref[index].astype(jnp.float32) * inverse).astype(jnp.bfloat16)
-            copies[3 * index].wait()
+        normed = []
+        for (ref, index), span in zip(blocks, spans):
+            normed.append((ref[index].astype(jnp.float32) * inverse).astype(jnp.bfloat16))
+        for step in range(pool_size):
+            copies[2 * step].wait()
             gate_values = gate_values + lax.dot_general(
-                rows, gate_ref[:, span], across, preferred_element_type=jnp.float32
-            )
-            copies[3 * index + 1].wait()
+                normed[step], gate_ref[:, spans[step]], across, preferred_element_type=jnp.float32
+            )
+            copies[2 * step + 1].wait()
             up_values = up_values + lax.dot_general(
-                rows, up_ref[:, span], across, preferred_element_type=jnp.float32
+                normed[step], up_ref[:, spans[step]], across, preferred_element_type=jnp.float32
             )
         active = (gate_values / (1.0 + jnp.exp(-gate_values)) * up_values).astype(jnp.bfloat16)
-        for index, span in enumerate(spans):
-            copies[3 * index + 2].wait()
+        for index in range(pool_size):
+            span = slice(index * block_cols, (index + 1) * block_cols)
+            down_copies[index].wait()
             out_ref[index] = jnp.dot(active, down_ref[:, span], preferred_element_type=jnp.float32).astype(
                 jnp.bfloat16
             )
 
     whole = pl.BlockSpec(memory_space=pltpu.VMEM)
+    hbm = pl.BlockSpec(memory_space=pltpu.HBM)
     return pl.pallas_call(
         body,
-        in_specs=[whole] + [pl.BlockSpec(memory_space=pltpu.HBM)] * 3,
+        in_specs=[whole] * len(states) + [hbm] * 3,
+        out_shape=jax.ShapeDtypeStruct((pool_size, prompts, block_cols), jnp.bfloat16),
         scratch_shapes=[
             pltpu.VMEM((hidden, width), gate_weight.dtype),
             pltpu.VMEM((hidden, width), up_weight.dtype),
             pltpu.VMEM((hidden, width), down_weight.dtype),
             pltpu.SemaphoreType.DMA((3, pool_size)),
         ],
-        out_shape=jax.ShapeDtypeStruct(state.shape, jnp.bfloat16),
         name="feed_forward",
         compiler_params=small_grant(48),
         cost_estimate=pl.CostEstimate(
             flops=6 * prompts * width * hidden, bytes_accessed=6 * width * hidden, transcendentals=prompts * hidden
         ),
-    )(state, gate_weight.T, up_weight.T, down_weight)
+    )(*states, in_hbm(gate_weight), in_hbm(up_weight), in_hbm(down_weight))
 
 
 def exchange(pieces):
@@ -537,7 +588,7 @@
     received = exchange(project(hidden_in, weights, pool_size, local_heads, group_size))
 
     pairs = prompts // 2
-    early = (5 * pairs) // 8
+    early = (6 * pairs) // 8
     paired_keys = key_cache.reshape((2, pairs) + key_cache.shape[1:])
     rotated = rope_keys(paired_keys, positions, 0, early, None)
     value_rows = value_cache.reshape(all_items, seq_local, HD)
@@ -565,7 +616,11 @@
     attn_out = heads_sum(project_out(attended, out_weight, prompts))
     hidden_cols = lax.dynamic_slice_in_dim(hidden_in, pool_index * block_cols, block_cols, 1)
     mid_state = (hidden_cols.astype(jnp.float32) + attn_out).astype(jnp.bfloat16)
-    pieces = exchange(feed_forward(gather(mid_state), gate_weight, up_weight, down_weight))
+    if pool_size <= 8 and pool_size % 2 == 0 and lax.axis_size("heads") == 2:
+        states = gather_by_halves(mid_state)
+    else:
+        states = (gather(mid_state),)
+    pieces = exchange(feed_forward(states, gate_weight.T, up_weight.T, down_weight, pool_size))
     mlp_cols = heads_sum(jnp.sum(pieces.astype(jnp.float32), 0))
     return (mid_state.astype(jnp.float32) + mlp_cols).astype(jnp.bfloat16)
 

time: 113 us -> 112 us (level)
  blocking collectives: 45.7 us -> 32.4 us
  starting transfers between devices: 12.3 us -> 19.1 us
  waiting for transfers between devices: 5.48 us -> 11.2 us
    all_to_all x4 -> x3, blocking collectives: 45.7 us -> 32.4 us  [exchange(): return lax.all_to_all(pieces, 'pool', 0, 0, tiled=True)]
    ppermute x0 -> x5, starting transfers between devices: none -> 5.78 us  [the longest x4 3.13 us: gather_by_halves(): parts.append(lax.ppermute(block, ('pool', 'heads'), pairs))]
    ppermute x0 -> x5, waiting for transfers between devices: none -> 5.66 us  [the longest x4 4.68 us: gather_by_halves(): parts.append(lax.ppermute(block, ('pool', 'heads'), pairs))]
  transfers between devices with their start and end apart: 4 -> 9, of which waited for: 4 -> 8; matrix products, arithmetic and copies ran while one was open for 1% -> 1% of each run, Pallas kernels for 12% -> 12%
where the time goes in v4:
time: 112 us; the launch traced here: 111 us
  Pallas kernels  45.7 us (41%)
  blocking collectives  32.4 us (29%)
  starting transfers between devices  19.1 us (17%)
  waiting for transfers between devices  11.2 us (10%)
  other arithmetic  1.92 us (2%)
    all_to_all x3, blocking collectives, exchange(): return lax.all_to_all(pieces, 'pool', 0, 0, tiled=True)  32.4 us
    pallas_call x1, Pallas kernels, feed_forward(): pl.pallas_call(body, in_specs=[whole] * len(states) + [hbm] * 3, out_shap...  14.9 us
    pallas_call x2, Pallas kernels, rope_keys(): pl.pallas_call(body, in_specs=[vmem, vmem, hbm] + [hbm for _ in partners]...  13.6 us
    all_to_all x2, starting transfers between devices, exchange(): return lax.all_to_all(pieces, 'pool', 0, 0, tiled=True)  13.2 us
    pallas_call x1, Pallas kernels, attend(): pl.pallas_call(body, in_specs=[pl.BlockSpec(memory_space=pltpu.SMEM), vme...  7.28 us
    pallas_call x1, Pallas kernels, project(): pl.pallas_call(body, in_specs=[hbm, hbm, hbm, hbm], out_specs=vmem, out_s...  5.28 us
    ppermute x4, waiting for transfers between devices, gather_by_halves(): parts.append(lax.ppermute(block, ('pool', 'heads'), pairs))  4.68 us
    pallas_call x1, Pallas kernels, project_out(): pl.pallas_call(body, in_specs=[vmem, pl.BlockSpec(memory_space=pltpu.HBM)...  3.74 us
  transfers between devices with their start and end apart: 9, of which 8 were waited for; matrix products, arithmetic and copies ran while one was open for 1% of the time, Pallas kernels for 12%

profile of v4, /device:TPU:0, one launch (start us, length us, event | category | flops | bytes accessed | tf_op | source)
XLA Modules:
  0.0 111.1 jit_solution(547794038477986956)
XLA Ops:
  0.0 0.0 copy-start.1
  0.0 5.3 %project.1 = f32[640,128]{1,0:T(8,128)} custom-call(bf16[16,8192]{1,0:T(8,128)(2,1)} %hidden_hbm.1, bf16[1024,4096]{1,0:T(8,128)(2,1)} %query_hbm.1, bf16[1024,512]{1,0:T(8,128)(2,1)} %key_hbm.1, bf16[1024,512]{1,0:T(8,128)(2,1)} %value_hbm.1), custom_call_target="tpu_custom_call" | custom-call | tf_op jit(solution)/shard_map/project/pallas_call | solution.py:209
  5.3 7.3 %all-to-all-start = ((f32[8,80,128]{2,1,0:T(8,128)}), f32[8,80,128]{2,1,0:T(8,128)S(1)}, u32[]{:S(2)}, u32[]{:S(2)}) async-start(f32[8,80,128]{2,1,0:T(8,128)} %bitcast.25), calls=%async_computation | async-start | bytes 655360 | tf_op jit(solution)/shard_map/all_to_all | solution.py:543
  12.6 0.0 copy-done.1
  12.7 0.6 broadcast_in_dim_tile.6.inverse_ref
  13.3 0.1 concatenate.15
  13.4 8.9 %rope_keys.2.refs_0_ = bf16[2,8,4,512,128]{4,3,2,1,0:T(8,128)(2,1)} custom-call(s32[3,16,512]{2,1,0:T(8,128)} %positions_ref.3, f32[1,128]{1,0:T(1,128)} %broadcast_in_dim_tile.6.inverse_ref, bf16[2,8,4,512,128]{4,3,2,1,0:T(8,128)(2,1)} %bitcast.20), custom_call_target="tpu_custom_call" | custom-call | tf_op jit(solution)/shard_map/rope_keys/pallas_call | solution.py:126
  22.3 0.1 and_select_fusion
  22.4 0.1 select_reduce_fusion.2
  22.5 0.2 fusion.3
  22.7 0.1 pad_maximum_fusion.1
  22.8 0.1 all-to-all-done.received_ref
  22.9 0.7 finish_rows.1
  23.6 5.9 %all-to-all-start.1 = ((bf16[8,80,128]{2,1,0:T(8,128)(2,1)}), bf16[8,80,128]{2,1,0:T(8,128)(2,1)S(1)}, u32[]{:S(2)}, u32[]{:S(2)}) async-start(bf16[8,80,128]{2,1,0:T(8,128)(2,1)} %finish_rows.1), calls=%async_computation.1 | async-start | bytes 327680 | tf_op jit(solution)/shard_map/all_to_all | solution.py:543
  29.5 0.0 copy-start
  29.5 4.7 %rope_keys.3 = bf16[2,8,4,512,128]{4,3,2,1,0:T(8,128)(2,1)} custom-call(s32[3,16,512]{2,1,0:T(8,128)} %positions_ref.3, f32[1,128]{1,0:T(1,128)} %broadcast_in_dim_tile.6.inverse_ref, bf16[2,8,4,512,128]{4,3,2,1,0:T(8,128)(2,1)} %bitcast.21, bf16[2,8,4,512,128]{4,3,2,1,0:T(8,128)(2,1)} %rope_keys.2.refs_0_), custom_call_target="tpu_custom_call", output_to_operand_aliasing={{}: (3, {})} | custom-call | tf_op jit(solution)/shard_map/rope_keys/pallas_call | solution.py:126
  34.2 2.9 %all-to-all-done.1.new_ref = bf16[8,80,128]{2,1,0:T(8,128)(2,1)S(1)} async-done(((bf16[8,80,128]{2,1,0:T(8,128)(2,1)}), bf16[8,80,128]{2,1,0:T(8,128)(2,1)S(1)}, u32[]{:S(2)}, u32[]{:S(2)}) %all-to-all-start.1) | async-done | bytes 163872 | tf_op jit(solution)/shard_map/all_to_all | solution.py:543
  37.1 0.0 copy-done
  37.1 7.3 %attend.1 = bf16[8,80,128]{2,1,0:T(8,128)(2,1)S(1)} custom-call(s32[16]{0:T(128)S(1)} %copy-done, bf16[8,80,128]{2,1,0:T(8,128)(2,1)S(1)} %all-to-all-done.1.new_ref, bf16[64,512,128]{2,1,0:T(8,128)(2,1)} %bitcast.19, bf16[64,512,128]{2,1,0:T(8,128)(2,1)} %bitcast.24), custom_call_target="tpu_custom_call" | custom-call | tf_op jit(solution)/shard_map/attend/pallas_call | solution.py:388
  44.4 10.5 %all_to_all.25.parts_ref = bf16[8,80,128]{2,1,0:T(8,128)(2,1)S(1)} all-to-all(bf16[8,80,128]{2,1,0:T(8,128)(2,1)S(1)} %attend.1), channel_id=1, replica_groups=mesh['groups'=2,'pool'=8,'heads'=2] {'pool'}, dimensions={0} | all-to-all | bytes 327680 | tf_op jit(solution)/shard_map/all_to_all | solution.py:543
  54.9 0.2 combine.1
  55.1 9.7 %all_to_all.26 = bf16[8,64,128]{2,1,0:T(8,128)(2,1)S(1)} all-to-all(bf16[8,64,128]{2,1,0:T(8,128)(2,1)S(1)} %combine.1), channel_id=1, replica_groups=mesh['groups'=2,'pool'=8,'heads'=2] {'pool'}, dimensions={0} | all-to-all | bytes 262144 | tf_op jit(solution)/shard_map/all_to_all | solution.py:543
  64.8 3.7 %project_out.1 = f32[16,1024]{1,0:T(8,128)S(1)} custom-call(bf16[512,128]{1,0:T(8,128)(2,1)S(1)} %bitcast.18, bf16[4096,1024]{1,0:T(8,128)(2,1)} %weight_hbm.1), custom_call_target="tpu_custom_call" | custom-call | tf_op jit(solution)/shard_map/project_out/pallas_call | solution.py:256
  68.6 0.1 collective-permute-start
  68.6 1.2 %collective-permute-done = f32[16,1024]{1,0:T(8,128)S(1)} collective-permute-done((f32[16,1024]{1,0:T(8,128)S(1)}, f32[16,1024]{1,0:T(8,128)S(1)}, u32[]{:S(2)}, u32[]{:S(2)}) %collective-permute-start) | collective-permute-done | bytes 65568 | tf_op jit(solution)/shard_map/ppermute | solution.py:556
  69.9 0.8 add_convert_fusion.1
  70.6 0.7 collective-permute-start.1
  71.3 0.6 collective-permute-start.4
  71.9 0.8 collective-permute-start.3
  72.7 1.1 collective-permute-start.2
  73.8 0.0 collective-permute-done.1
  73.8 1.5 %collective-permute-done.4 = bf16[16,1024]{1,0:T(8,128)(2,1)S(1)} collective-permute-done((bf16[16,1024]{1,0:T(8,128)(2,1)S(1)}, bf16[16,1024]{1,0:T(8,128)(2,1)S(1)}, u32[]{:S(2)}, u32[]{:S(2)}) %collective-permute-start.4) | collective-permute-done | bytes 32800 | tf_op jit(solution)/shard_map/ppermute | solution.py:450
  75.3 1.5 %collective-permute-done.3 = bf16[16,1024]{1,0:T(8,128)(2,1)S(1)} collective-permute-done((bf16[16,1024]{1,0:T(8,128)(2,1)S(1)}, bf16[16,1024]{1,0:T(8,128)(2,1)S(1)}, u32[]{:S(2)}, u32[]{:S(2)}) %collective-permute-start.3) | collective-permute-done | bytes 32800 | tf_op jit(solution)/shard_map/ppermute | solution.py:450
  76.8 1.7 %collective-permute-done.2 = bf16[16,1024]{1,0:T(8,128)(2,1)S(1)} collective-permute-done((bf16[16,1024]{1,0:T(8,128)(2,1)S(1)}, bf16[16,1024]{1,0:T(8,128)(2,1)S(1)}, u32[]{:S(2)}, u32[]{:S(2)}) %collective-permute-start.2) | collective-permute-done | bytes 32800 | tf_op jit(solution)/shard_map/ppermute | solution.py:450
  78.5 2.7 %collective-permute-start.5 = (bf16[4,16,1024]{2,1,0:T(8,128)(2,1)S(1)}, bf16[4,16,1024]{2,1,0:T(8,128)(2,1)S(1)}, u32[]{:S(2)}, u32[]{:S(2)}) collective-permute-start(bf16[4,16,1024]{2,1,0:T(8,128)(2,1)S(1)} %pad_maximum_fusion.refs_0_), channel_id=1, source_target_pairs={{0,1},{1,0},{2,3},{3,2},{4,5},{5,4},{6,7},{7,6},{8,9},{9,8},{10,11... | collective-permute-start | bytes 393224 | tf_op jit(solution)/shard_map/ppermute | solution.py:453
  81.2 1.0 collective-permute-done.5.refs_1_
  82.1 14.9 %feed_forward.1 = bf16[8,16,1024]{2,1,0:T(8,128)(2,1)S(1)} custom-call(bf16[4,16,1024]{2,1,0:T(8,128)(2,1)S(1)} %pad_maximum_fusion.refs_0_, bf16[4,16,1024]{2,1,0:T(8,128)(2,1)S(1)} %collective-permute-done.5.refs_1_, bf16[928,8192]{1,0:T(8,128)(2,1)} %bitcast.22, bf16[928,8192]{1,0:T(8,128)(2,1)} %bitcast.23, bf16[928,8192]{1,0:T(8,128)(2,1)} %refs_4_.1), custom_call_target="tpu_custom_call" | custom-call | flops 729808896 | bytes 45613056 | tf_op jit(solution)/shard_map/feed_forward/pallas_call | solution.py:524
  97.0 12.1 %all_to_all.27 = bf16[8,16,1024]{2,1,0:T(8,128)(2,1)S(1)} all-to-all(bf16[8,16,1024]{2,1,0:T(8,128)(2,1)S(1)} %feed_forward.1), channel_id=1, replica_groups=mesh['groups'=2,'pool'=8,'heads'=2] {'pool'}, dimensions={0} | all-to-all | bytes 524288 | tf_op jit(solution)/shard_map/all_to_all | solution.py:543
  109.2 0.1 collective-permute-start.6
  109.3 1.2 %collective-permute-done.6 = f32[16,1024]{1,0:T(8,128)S(1)} collective-permute-done((f32[16,1024]{1,0:T(8,128)S(1)}, f32[16,1024]{1,0:T(8,128)S(1)}, u32[]{:S(2)}, u32[]{:S(2)}) %collective-permute-start.6) | collective-permute-done | bytes 65568 | tf_op jit(solution)/shard_map/ppermute | solution.py:556
  110.5 0.6 add_convert_fusion
  (12 shorter events, 0.1 us)
Async XLA Ops:
  0.0 12.6 %copy-start.1 = (s32[3,16]{1,0:T(4,128)S(1)}, s32[3,16]{1,0:T(4,128)}, u32[]{:S(2)}) copy-start(s32[3,16]{1,0:T(4,128)} %param.17) | copy-start | bytes 580
  5.3 17.6 %all-to-all-start = ((f32[8,80,128]{2,1,0:T(8,128)}), f32[8,80,128]{2,1,0:T(8,128)S(1)}, u32[]{:S(2)}, u32[]{:S(2)}) async-start(f32[8,80,128]{2,1,0:T(8,128)} %bitcast.25), calls=%async_computation | async-start | bytes 655360 | tf_op jit(solution)/shard_map/all_to_all | solution.py:543
  23.6 13.4 %all-to-all-start.1 = ((bf16[8,80,128]{2,1,0:T(8,128)(2,1)}), bf16[8,80,128]{2,1,0:T(8,128)(2,1)S(1)}, u32[]{:S(2)}, u32[]{:S(2)}) async-start(bf16[8,80,128]{2,1,0:T(8,128)(2,1)} %finish_rows.1), calls=%async_computation.1 | async-start | bytes 327680 | tf_op jit(solution)/shard_map/all_to_all | solution.py:543
  29.5 7.6 %copy-start = (s32[16]{0:T(128)S(1)}, s32[16]{0:T(128)}, u32[]{:S(2)}) copy-start(s32[16]{0:T(128)} %lengths_ref.1) | copy-start | bytes 196
  68.6 1.3 %collective-permute-start = (f32[16,1024]{1,0:T(8,128)S(1)}, f32[16,1024]{1,0:T(8,128)S(1)}, u32[]{:S(2)}, u32[]{:S(2)}) collective-permute-start(f32[16,1024]{1,0:T(8,128)S(1)} %project_out.1), channel_id=1, source_target_pairs={{0,1},{1,0},{2,3},{3,2},{4,5},{5,4},{6,7},{7,6},{8,9},{9,8},{10,11... | collective-permute-start | bytes 196616 | tf_op jit(solution)/shard_map/ppermute | solution.py:556
  70.6 3.1 %collective-permute-start.1 = (bf16[16,1024]{1,0:T(8,128)(2,1)S(1)}, bf16[16,1024]{1,0:T(8,128)(2,1)S(1)}, u32[]{:S(2)}, u32[]{:S(2)}) collective-permute-start(bf16[16,1024]{1,0:T(8,128)(2,1)S(1)} %add_convert_fusion.1), channel_id=1, source_target_pairs={{1,3},{3,1},{5,7},{7,5},{9,11},{11,9},{13,15},{15,13},{17,19},{19,... | collective-permute-start | bytes 98312 | tf_op jit(solution)/shard_map/ppermute | solution.py:450
  71.3 4.0 %collective-permute-start.4 = (bf16[16,1024]{1,0:T(8,128)(2,1)S(1)}, bf16[16,1024]{1,0:T(8,128)(2,1)S(1)}, u32[]{:S(2)}, u32[]{:S(2)}) collective-permute-start(bf16[16,1024]{1,0:T(8,128)(2,1)S(1)} %add_convert_fusion.1), channel_id=1, source_target_pairs={{0,12},{1,15},{2,14},{3,13},{4,0},{5,3},{6,2},{7,1},{8,4},{9,7},{1... | collective-permute-start | bytes 98312 | tf_op jit(solution)/shard_map/ppermute | solution.py:450
  71.9 4.8 %collective-permute-start.3 = (bf16[16,1024]{1,0:T(8,128)(2,1)S(1)}, bf16[16,1024]{1,0:T(8,128)(2,1)S(1)}, u32[]{:S(2)}, u32[]{:S(2)}) collective-permute-start(bf16[16,1024]{1,0:T(8,128)(2,1)S(1)} %add_convert_fusion.1), channel_id=1, source_target_pairs={{0,8},{1,11},{2,10},{3,9},{4,12},{5,15},{6,14},{7,13},{8,0},{9,3},... | collective-permute-start | bytes 98312 | tf_op jit(solution)/shard_map/ppermute | solution.py:450
  72.7 5.8 %collective-permute-start.2 = (bf16[16,1024]{1,0:T(8,128)(2,1)S(1)}, bf16[16,1024]{1,0:T(8,128)(2,1)S(1)}, u32[]{:S(2)}, u32[]{:S(2)}) collective-permute-start(bf16[16,1024]{1,0:T(8,128)(2,1)S(1)} %add_convert_fusion.1), channel_id=1, source_target_pairs={{0,4},{1,7},{2,6},{3,5},{4,8},{5,11},{6,10},{7,9},{8,12},{9,15},{1... | collective-permute-start | bytes 98312 | tf_op jit(solution)/shard_map/ppermute | solution.py:450
  78.5 3.6 %collective-permute-start.5 = (bf16[4,16,1024]{2,1,0:T(8,128)(2,1)S(1)}, bf16[4,16,1024]{2,1,0:T(8,128)(2,1)S(1)}, u32[]{:S(2)}, u32[]{:S(2)}) collective-permute-start(bf16[4,16,1024]{2,1,0:T(8,128)(2,1)S(1)} %pad_maximum_fusion.refs_0_), channel_id=1, source_target_pairs={{0,1},{1,0},{2,3},{3,2},{4,5},{5,4},{6,7},{7,6},{8,9},{9,8},{10,11... | collective-permute-start | bytes 393224 | tf_op jit(solution)/shard_map/ppermute | solution.py:453
  109.2 1.3 %collective-permute-start.6 = (f32[16,1024]{1,0:T(8,128)S(1)}, f32[16,1024]{1,0:T(8,128)S(1)}, u32[]{:S(2)}, u32[]{:S(2)}) collective-permute-start(f32[16,1024]{1,0:T(8,128)S(1)} %convert_reduce_fusion), channel_id=1, source_target_pairs={{0,1},{1,0},{2,3},{3,2},{4,5},{5,4},{6,7},{7,6},{8,9},{9,8},{10,11... | collective-permute-start | bytes 196616 | tf_op jit(solution)/shard_map/ppermute | solution.py:556

commit v5 on v4

--- a/solution.py
+++ b/solution.py
@@ -2,6 +2,7 @@
 
 import jax
 import jax.numpy as jnp
+import numpy as np
 from jax import lax
 from jax.experimental import pallas as pl
 from jax.experimental.pallas import tpu as pltpu
@@ -32,8 +33,9 @@
 
 
 def frequencies():
-    column = jnp.arange(HD // 2)
-    return jnp.exp(column.astype(jnp.float32) * (-2.0 * math.log(THETA) / HD))
+    column = np.arange(HD // 2, dtype=np.float32)
+    exponents = column * np.float32(-2.0 * math.log(THETA) / HD)
+    return np.exp(exponents.astype(np.float64)).astype(np.float32)
 
 
 def sections():
@@ -56,7 +58,7 @@
     low_bits = 6
     chunk = min(slots, 64)
     count = last_pair - first_pair
-    inverse = jnp.tile(frequencies(), 2)[None]
+    inverse = jnp.asarray(np.tile(frequencies(), 2)[None])
 
     def body(positions_ref, inverse_ref, key_hbm, *refs):
         out_hbm, key_ref, out_ref, chosen_ref, cos_ref, sin_ref, sems = refs[-7:]

time: 112 us -> 111 us (level)
  transfers between devices with their start and end apart: 9 -> 9, of which waited for: 8 -> 8; matrix products, arithmetic and copies ran while one was open for 1% -> 0% of each run, Pallas kernels for 12% -> 12%
where the time goes in v5:
time: 111 us
  Pallas kernels  45.8 us (41%)
  blocking collectives  32.4 us (29%)
  starting transfers between devices  18.5 us (17%)
  waiting for transfers between devices  11.7 us (11%)
  other arithmetic  1.92 us (2%)
    all_to_all x3, blocking collectives, exchange(): return lax.all_to_all(pieces, 'pool', 0, 0, tiled=True)  32.4 us
    pallas_call x1, Pallas kernels, feed_forward(): pl.pallas_call(body, in_specs=[whole] * len(states) + [hbm] * 3, out_shap...  14.9 us
    pallas_call x2, Pallas kernels, rope_keys(): pl.pallas_call(body, in_specs=[vmem, vmem, hbm] + [hbm for _ in partners]...  13.6 us
    all_to_all x2, starting transfers between devices, exchange(): return lax.all_to_all(pieces, 'pool', 0, 0, tiled=True)  12.6 us
    pallas_call x1, Pallas kernels, attend(): pl.pallas_call(body, in_specs=[pl.BlockSpec(memory_space=pltpu.SMEM), vme...  7.28 us
    pallas_call x1, Pallas kernels, project(): pl.pallas_call(body, in_specs=[hbm, hbm, hbm, hbm], out_specs=vmem, out_s...  5.3 us
    ppermute x4, waiting for transfers between devices, gather_by_halves(): parts.append(lax.ppermute(block, ('pool', 'heads'), pairs))  4.68 us
    pallas_call x1, Pallas kernels, project_out(): pl.pallas_call(body, in_specs=[vmem, pl.BlockSpec(memory_space=pltpu.HBM)...  3.74 us
  transfers between devices with their start and end apart: 9, of which 8 were waited for; matrix products, arithmetic and copies ran while one was open for 0% of the time, Pallas kernels for 12%

profile of v5, /device:TPU:0, one launch (start us, length us, event | category | flops | bytes accessed | tf_op | source)
XLA Modules:
  0.0 110.6 jit_solution(4598121971325456720)
XLA Ops:
  0.0 0.0 copy-start.1
  0.0 5.3 %project.1 = f32[640,128]{1,0:T(8,128)} custom-call(bf16[16,8192]{1,0:T(8,128)(2,1)} %hidden_hbm.1, bf16[1024,4096]{1,0:T(8,128)(2,1)} %query_hbm.1, bf16[1024,512]{1,0:T(8,128)(2,1)} %key_hbm.1, bf16[1024,512]{1,0:T(8,128)(2,1)} %value_hbm.1), custom_call_target="tpu_custom_call" | custom-call | tf_op jit(solution)/shard_map/project/pallas_call | solution.py:211
  5.3 7.3 %all-to-all-start = ((f32[8,80,128]{2,1,0:T(8,128)}), f32[8,80,128]{2,1,0:T(8,128)S(1)}, u32[]{:S(2)}, u32[]{:S(2)}) async-start(f32[8,80,128]{2,1,0:T(8,128)} %bitcast.25), calls=%async_computation | async-start | bytes 655360 | tf_op jit(solution)/shard_map/all_to_all | solution.py:545
  12.6 0.0 copy-done.1
  12.7 0.1 concatenate.15
  12.8 0.0 copy-start.2
  12.8 9.0 %rope_keys.2.refs_0_ = bf16[2,8,4,512,128]{4,3,2,1,0:T(8,128)(2,1)} custom-call(s32[3,16,512]{2,1,0:T(8,128)} %positions_ref.3, f32[1,128]{1,0:T(1,128)} %constant.77.clone.inverse_ref, bf16[2,8,4,512,128]{4,3,2,1,0:T(8,128)(2,1)} %bitcast.20), custom_call_target="tpu_custom_call" | custom-call | tf_op jit(solution)/shard_map/rope_keys/pallas_call | solution.py:128
  21.8 0.1 and_select_fusion
  21.9 0.1 select_reduce_fusion.2
  21.9 0.0 copy-done.2
  22.0 0.2 fusion.3
  22.1 0.1 pad_maximum_fusion.1
  22.2 0.7 all-to-all-done.received_ref
  22.9 0.8 finish_rows.1
  23.7 5.3 %all-to-all-start.1 = ((bf16[8,80,128]{2,1,0:T(8,128)(2,1)}), bf16[8,80,128]{2,1,0:T(8,128)(2,1)S(1)}, u32[]{:S(2)}, u32[]{:S(2)}) async-start(bf16[8,80,128]{2,1,0:T(8,128)(2,1)} %finish_rows.1), calls=%async_computation.1 | async-start | bytes 327680 | tf_op jit(solution)/shard_map/all_to_all | solution.py:545
  29.0 0.0 copy-start
  29.0 4.7 %rope_keys.3 = bf16[2,8,4,512,128]{4,3,2,1,0:T(8,128)(2,1)} custom-call(s32[3,16,512]{2,1,0:T(8,128)} %positions_ref.3, f32[1,128]{1,0:T(1,128)} %constant.77.clone.inverse_ref, bf16[2,8,4,512,128]{4,3,2,1,0:T(8,128)(2,1)} %bitcast.21, bf16[2,8,4,512,128]{4,3,2,1,0:T(8,128)(2,1)} %rope_keys.2.refs_0_), custom_call_target="tpu_custom_call", output_to_operand_aliasing={{}: (3, {})} | custom-call | tf_op jit(solution)/shard_map/rope_keys/pallas_call | solution.py:128
  33.7 2.9 %all-to-all-done.1.new_ref = bf16[8,80,128]{2,1,0:T(8,128)(2,1)S(1)} async-done(((bf16[8,80,128]{2,1,0:T(8,128)(2,1)}), bf16[8,80,128]{2,1,0:T(8,128)(2,1)S(1)}, u32[]{:S(2)}, u32[]{:S(2)}) %all-to-all-start.1) | async-done | bytes 163872 | tf_op jit(solution)/shard_map/all_to_all | solution.py:545
  36.6 0.0 copy-done
  36.6 7.3 %attend.1 = bf16[8,80,128]{2,1,0:T(8,128)(2,1)S(1)} custom-call(s32[16]{0:T(128)S(1)} %copy-done, bf16[8,80,128]{2,1,0:T(8,128)(2,1)S(1)} %all-to-all-done.1.new_ref, bf16[64,512,128]{2,1,0:T(8,128)(2,1)} %bitcast.19, bf16[64,512,128]{2,1,0:T(8,128)(2,1)} %bitcast.24), custom_call_target="tpu_custom_call" | custom-call | tf_op jit(solution)/shard_map/attend/pallas_call | solution.py:390
  43.9 10.5 %all_to_all.25.parts_ref = bf16[8,80,128]{2,1,0:T(8,128)(2,1)S(1)} all-to-all(bf16[8,80,128]{2,1,0:T(8,128)(2,1)S(1)} %attend.1), channel_id=1, replica_groups=mesh['groups'=2,'pool'=8,'heads'=2] {'pool'}, dimensions={0} | all-to-all | bytes 327680 | tf_op jit(solution)/shard_map/all_to_all | solution.py:545
  54.3 0.2 combine.1
  54.5 9.7 %all_to_all.26 = bf16[8,64,128]{2,1,0:T(8,128)(2,1)S(1)} all-to-all(bf16[8,64,128]{2,1,0:T(8,128)(2,1)S(1)} %combine.1), channel_id=1, replica_groups=mesh['groups'=2,'pool'=8,'heads'=2] {'pool'}, dimensions={0} | all-to-all | bytes 262144 | tf_op jit(solution)/shard_map/all_to_all | solution.py:545
  64.3 3.7 %project_out.1 = f32[16,1024]{1,0:T(8,128)S(1)} custom-call(bf16[512,128]{1,0:T(8,128)(2,1)S(1)} %bitcast.18, bf16[4096,1024]{1,0:T(8,128)(2,1)} %weight_hbm.1), custom_call_target="tpu_custom_call" | custom-call | tf_op jit(solution)/shard_map/project_out/pallas_call | solution.py:258
  68.0 0.1 collective-permute-start
  68.1 1.2 %collective-permute-done = f32[16,1024]{1,0:T(8,128)S(1)} collective-permute-done((f32[16,1024]{1,0:T(8,128)S(1)}, f32[16,1024]{1,0:T(8,128)S(1)}, u32[]{:S(2)}, u32[]{:S(2)}) %collective-permute-start) | collective-permute-done | bytes 65568 | tf_op jit(solution)/shard_map/ppermute | solution.py:558
  69.4 0.8 add_convert_fusion.1
  70.1 0.7 collective-permute-start.1
  70.8 0.6 collective-permute-start.4
  71.4 0.8 collective-permute-start.3
  72.2 1.1 collective-permute-start.2
  73.3 0.0 collective-permute-done.1
  73.3 1.5 %collective-permute-done.4 = bf16[16,1024]{1,0:T(8,128)(2,1)S(1)} collective-permute-done((bf16[16,1024]{1,0:T(8,128)(2,1)S(1)}, bf16[16,1024]{1,0:T(8,128)(2,1)S(1)}, u32[]{:S(2)}, u32[]{:S(2)}) %collective-permute-start.4) | collective-permute-done | bytes 32800 | tf_op jit(solution)/shard_map/ppermute | solution.py:452
  74.8 1.5 %collective-permute-done.3 = bf16[16,1024]{1,0:T(8,128)(2,1)S(1)} collective-permute-done((bf16[16,1024]{1,0:T(8,128)(2,1)S(1)}, bf16[16,1024]{1,0:T(8,128)(2,1)S(1)}, u32[]{:S(2)}, u32[]{:S(2)}) %collective-permute-start.3) | collective-permute-done | bytes 32800 | tf_op jit(solution)/shard_map/ppermute | solution.py:452
  76.2 1.7 %collective-permute-done.2 = bf16[16,1024]{1,0:T(8,128)(2,1)S(1)} collective-permute-done((bf16[16,1024]{1,0:T(8,128)(2,1)S(1)}, bf16[16,1024]{1,0:T(8,128)(2,1)S(1)}, u32[]{:S(2)}, u32[]{:S(2)}) %collective-permute-start.2) | collective-permute-done | bytes 32800 | tf_op jit(solution)/shard_map/ppermute | solution.py:452
  78.0 2.7 %collective-permute-start.5 = (bf16[4,16,1024]{2,1,0:T(8,128)(2,1)S(1)}, bf16[4,16,1024]{2,1,0:T(8,128)(2,1)S(1)}, u32[]{:S(2)}, u32[]{:S(2)}) collective-permute-start(bf16[4,16,1024]{2,1,0:T(8,128)(2,1)S(1)} %pad_maximum_fusion.refs_0_), channel_id=1, source_target_pairs={{0,1},{1,0},{2,3},{3,2},{4,5},{5,4},{6,7},{7,6},{8,9},{9,8},{10,11... | collective-permute-start | bytes 393224 | tf_op jit(solution)/shard_map/ppermute | solution.py:455
  80.6 1.0 collective-permute-done.5.refs_1_
  81.6 14.9 %feed_forward.1 = bf16[8,16,1024]{2,1,0:T(8,128)(2,1)S(1)} custom-call(bf16[4,16,1024]{2,1,0:T(8,128)(2,1)S(1)} %pad_maximum_fusion.refs_0_, bf16[4,16,1024]{2,1,0:T(8,128)(2,1)S(1)} %collective-permute-done.5.refs_1_, bf16[928,8192]{1,0:T(8,128)(2,1)} %bitcast.22, bf16[928,8192]{1,0:T(8,128)(2,1)} %bitcast.23, bf16[928,8192]{1,0:T(8,128)(2,1)} %refs_4_.1), custom_call_target="tpu_custom_call" | custom-call | flops 729808896 | bytes 45613056 | tf_op jit(solution)/shard_map/feed_forward/pallas_call | solution.py:526
  96.5 12.1 %all_to_all.27 = bf16[8,16,1024]{2,1,0:T(8,128)(2,1)S(1)} all-to-all(bf16[8,16,1024]{2,1,0:T(8,128)(2,1)S(1)} %feed_forward.1), channel_id=1, replica_groups=mesh['groups'=2,'pool'=8,'heads'=2] {'pool'}, dimensions={0} | all-to-all | bytes 524288 | tf_op jit(solution)/shard_map/all_to_all | solution.py:545
  108.7 0.1 collective-permute-start.6
  108.8 1.2 %collective-permute-done.6 = f32[16,1024]{1,0:T(8,128)S(1)} collective-permute-done((f32[16,1024]{1,0:T(8,128)S(1)}, f32[16,1024]{1,0:T(8,128)S(1)}, u32[]{:S(2)}, u32[]{:S(2)}) %collective-permute-start.6) | collective-permute-done | bytes 65568 | tf_op jit(solution)/shard_map/ppermute | solution.py:558
  110.0 0.6 add_convert_fusion
  (10 shorter events, 0.1 us)
Async XLA Ops:
  0.0 12.6 %copy-start.1 = (s32[3,16]{1,0:T(4,128)S(1)}, s32[3,16]{1,0:T(4,128)}, u32[]{:S(2)}) copy-start(s32[3,16]{1,0:T(4,128)} %param.20) | copy-start | bytes 580
  5.3 17.6 %all-to-all-start = ((f32[8,80,128]{2,1,0:T(8,128)}), f32[8,80,128]{2,1,0:T(8,128)S(1)}, u32[]{:S(2)}, u32[]{:S(2)}) async-start(f32[8,80,128]{2,1,0:T(8,128)} %bitcast.25), calls=%async_computation | async-start | bytes 655360 | tf_op jit(solution)/shard_map/all_to_all | solution.py:545
  12.8 9.2 %copy-start.2 = (f32[64]{0:T(128)S(1)}, f32[64]{0:T(128)}, u32[]{:S(2)}) copy-start(f32[64]{0:T(128)} %constant.78.clone) | copy-start | bytes 772
  23.7 12.9 %all-to-all-start.1 = ((bf16[8,80,128]{2,1,0:T(8,128)(2,1)}), bf16[8,80,128]{2,1,0:T(8,128)(2,1)S(1)}, u32[]{:S(2)}, u32[]{:S(2)}) async-start(bf16[8,80,128]{2,1,0:T(8,128)(2,1)} %finish_rows.1), calls=%async_computation.1 | async-start | bytes 327680 | tf_op jit(solution)/shard_map/all_to_all | solution.py:545
  29.0 7.6 %copy-start = (s32[16]{0:T(128)S(1)}, s32[16]{0:T(128)}, u32[]{:S(2)}) copy-start(s32[16]{0:T(128)} %lengths_ref.1) | copy-start | bytes 196
  68.0 1.3 %collective-permute-start = (f32[16,1024]{1,0:T(8,128)S(1)}, f32[16,1024]{1,0:T(8,128)S(1)}, u32[]{:S(2)}, u32[]{:S(2)}) collective-permute-start(f32[16,1024]{1,0:T(8,128)S(1)} %project_out.1), channel_id=1, source_target_pairs={{0,1},{1,0},{2,3},{3,2},{4,5},{5,4},{6,7},{7,6},{8,9},{9,8},{10,11... | collective-permute-start | bytes 196616 | tf_op jit(solution)/shard_map/ppermute | solution.py:558
  70.1 3.1 %collective-permute-start.1 = (bf16[16,1024]{1,0:T(8,128)(2,1)S(1)}, bf16[16,1024]{1,0:T(8,128)(2,1)S(1)}, u32[]{:S(2)}, u32[]{:S(2)}) collective-permute-start(bf16[16,1024]{1,0:T(8,128)(2,1)S(1)} %add_convert_fusion.1), channel_id=1, source_target_pairs={{1,3},{3,1},{5,7},{7,5},{9,11},{11,9},{13,15},{15,13},{17,19},{19,... | collective-permute-start | bytes 98312 | tf_op jit(solution)/shard_map/ppermute | solution.py:452
  70.8 4.0 %collective-permute-start.4 = (bf16[16,1024]{1,0:T(8,128)(2,1)S(1)}, bf16[16,1024]{1,0:T(8,128)(2,1)S(1)}, u32[]{:S(2)}, u32[]{:S(2)}) collective-permute-start(bf16[16,1024]{1,0:T(8,128)(2,1)S(1)} %add_convert_fusion.1), channel_id=1, source_target_pairs={{0,12},{1,15},{2,14},{3,13},{4,0},{5,3},{6,2},{7,1},{8,4},{9,7},{1... | collective-permute-start | bytes 98312 | tf_op jit(solution)/shard_map/ppermute | solution.py:452
  71.4 4.8 %collective-permute-start.3 = (bf16[16,1024]{1,0:T(8,128)(2,1)S(1)}, bf16[16,1024]{1,0:T(8,128)(2,1)S(1)}, u32[]{:S(2)}, u32[]{:S(2)}) collective-permute-start(bf16[16,1024]{1,0:T(8,128)(2,1)S(1)} %add_convert_fusion.1), channel_id=1, source_target_pairs={{0,8},{1,11},{2,10},{3,9},{4,12},{5,15},{6,14},{7,13},{8,0},{9,3},... | collective-permute-start | bytes 98312 | tf_op jit(solution)/shard_map/ppermute | solution.py:452
  72.2 5.8 %collective-permute-start.2 = (bf16[16,1024]{1,0:T(8,128)(2,1)S(1)}, bf16[16,1024]{1,0:T(8,128)(2,1)S(1)}, u32[]{:S(2)}, u32[]{:S(2)}) collective-permute-start(bf16[16,1024]{1,0:T(8,128)(2,1)S(1)} %add_convert_fusion.1), channel_id=1, source_target_pairs={{0,4},{1,7},{2,6},{3,5},{4,8},{5,11},{6,10},{7,9},{8,12},{9,15},{1... | collective-permute-start | bytes 98312 | tf_op jit(solution)/shard_map/ppermute | solution.py:452
  78.0 3.6 %collective-permute-start.5 = (bf16[4,16,1024]{2,1,0:T(8,128)(2,1)S(1)}, bf16[4,16,1024]{2,1,0:T(8,128)(2,1)S(1)}, u32[]{:S(2)}, u32[]{:S(2)}) collective-permute-start(bf16[4,16,1024]{2,1,0:T(8,128)(2,1)S(1)} %pad_maximum_fusion.refs_0_), channel_id=1, source_target_pairs={{0,1},{1,0},{2,3},{3,2},{4,5},{5,4},{6,7},{7,6},{8,9},{9,8},{10,11... | collective-permute-start | bytes 393224 | tf_op jit(solution)/shard_map/ppermute | solution.py:455
  108.7 1.3 %collective-permute-start.6 = (f32[16,1024]{1,0:T(8,128)S(1)}, f32[16,1024]{1,0:T(8,128)S(1)}, u32[]{:S(2)}, u32[]{:S(2)}) collective-permute-start(f32[16,1024]{1,0:T(8,128)S(1)} %convert_reduce_fusion), channel_id=1, source_target_pairs={{0,1},{1,0},{2,3},{3,2},{4,5},{5,4},{6,7},{7,6},{8,9},{9,8},{10,11... | collective-permute-start | bytes 196616 | tf_op jit(solution)/shard_map/ppermute | solution.py:558
